TPU v7x, 8 devices: a whole 2x2x1 slice. The times are simulated.
8 devices in a mesh: fsdp: 8 (over z, y, x, core).
Axes of the slice: x: 2, y: 2, z: 1, core: 2. Of those that a mesh axis runs over, the one named last changes fastest.
Arguments:
- x_saved: bfloat16 [2, 16, 1536, 1536], P(None, 'fsdp')
- grad_out: bfloat16 [16, 1536, 1536], P('fsdp')
- x_next: bfloat16 [16, 1536, 1536], P('fsdp')
- w_up: bfloat16 [2, 1536, 6144], replicated
- w_down: bfloat16 [2, 6144, 1536], replicated
- gacc_up: float32 [2, 1536, 6144], P(None, 'fsdp')
- gacc_down: float32 [2, 6144, 1536], P(None, 'fsdp')
- master_up: float32 [2, 1536, 6144], P(None, 'fsdp')
- master_down: float32 [2, 6144, 1536], P(None, 'fsdp')
- mom1_up: float32 [2, 1536, 6144], P(None, 'fsdp')
- mom1_down: float32 [2, 6144, 1536], P(None, 'fsdp')
- mom2_up: float32 [2, 1536, 6144], P(None, 'fsdp')
- mom2_down: float32 [2, 6144, 1536], P(None, 'fsdp')
Outputs:
- output 1: bfloat16 [16, 1536, 1536], P('fsdp')
- output 2: float32 [2, 1536, 6144], P(None, 'fsdp')
- output 3: float32 [2, 6144, 1536], P(None, 'fsdp')
- output 4: float32 [2, 1536, 6144], P(None, 'fsdp')
- output 5: float32 [2, 6144, 1536], P(None, 'fsdp')
- output 6: float32 [2, 1536, 6144], P(None, 'fsdp')
- output 7: float32 [2, 6144, 1536], P(None, 'fsdp')
All inputs are finite; a program needn't handle non-finite values.
Results may differ from a plain program's by a relative error of at most 0.00830136.
Values are sent between devices in bfloat16 or wider.
A program may use at most 1 GiB of HBM per device.

v0:
```python
import math
import jax
import jax.numpy as jnp
from jax import lax
from jax.sharding import PartitionSpec as P

LEARN_RATE = 0.001
BETA_ONE = 0.9
BETA_TWO = 0.95
ADAM_EPS = 1e-8
WEIGHT_DECAY = 0.1
ADAM_STEP = 3
MICRO_STEPS = 2


def gelu_fn(pre_act):
    return jax.nn.gelu(pre_act, approximate=True)


def adamw_update(master_old, mom_one, mom_two, grad_clip):
    mom_one_new = BETA_ONE * mom_one + (1.0 - BETA_ONE) * grad_clip
    mom_two_new = BETA_TWO * mom_two + (1.0 - BETA_TWO) * grad_clip * grad_clip
    first_hat = mom_one_new / (1.0 - BETA_ONE ** ADAM_STEP)
    second_hat = mom_two_new / (1.0 - BETA_TWO ** ADAM_STEP)
    master_new = master_old - LEARN_RATE * (first_hat / (jnp.sqrt(second_hat) + ADAM_EPS) + WEIGHT_DECAY * master_old)
    return master_new, mom_one_new, mom_two_new


def reduce_rows(part_grad, n_dev):
    received = lax.all_to_all(part_grad, "fsdp", 0, 0, tiled=True)
    return jnp.sum(received.reshape(n_dev, -1, part_grad.shape[1]), axis=0, dtype=jnp.float32)


def backward_update(x_saved, grad_out, w_up, w_down, gacc_up, gacc_down, master_up, master_down, mom1_up, mom1_down, mom2_up, mom2_down, n_dev):
    layers, model_width, ff_width = w_up.shape
    clip_norm = 0.1 * math.sqrt(2 * layers * model_width * ff_width)
    x_tokens = x_saved.reshape(layers, -1, model_width)
    grad_cur = grad_out.reshape(-1, model_width)
    sums_up = []
    sums_down = []
    for layer_idx in range(layers - 1, -1, -1):
        x_in = x_tokens[layer_idx]
        pre_act = jnp.dot(x_in, w_up[layer_idx], preferred_element_type=jnp.float32)
        hidden_act, gelu_vjp = jax.vjp(gelu_fn, pre_act)
        d_act = lax.dot_general(grad_cur, w_down[layer_idx], (((1,), (1,)), ((), ())), preferred_element_type=jnp.float32)
        d_pre = gelu_vjp(d_act)[0].astype(jnp.bfloat16)
        part_down = lax.dot_general(hidden_act.astype(jnp.bfloat16), grad_cur, (((0,), (0,)), ((), ())), preferred_element_type=jnp.float32).astype(jnp.bfloat16)
        part_up = lax.dot_general(x_in, d_pre, (((0,), (0,)), ((), ())), preferred_element_type=jnp.float32).astype(jnp.bfloat16)
        if layer_idx > 0:
            grad_cur = (grad_cur.astype(jnp.float32) + lax.dot_general(d_pre, w_up[layer_idx], (((1,), (1,)), ((), ())), preferred_element_type=jnp.float32)).astype(jnp.bfloat16)
        sums_down.append(reduce_rows(part_down, n_dev))
        sums_up.append(reduce_rows(part_up, n_dev))
    grad_up = (gacc_up + jnp.stack(sums_up[::-1])) / MICRO_STEPS
    grad_down = (gacc_down + jnp.stack(sums_down[::-1])) / MICRO_STEPS
    local_sq = jnp.sum(grad_up * grad_up) + jnp.sum(grad_down * grad_down)
    clip_factor = jnp.minimum(1.0, clip_norm / jnp.sqrt(lax.psum(local_sq, "fsdp")))
    new_up = adamw_update(master_up, mom1_up, mom2_up, grad_up * clip_factor)
    new_down = adamw_update(master_down, mom1_down, mom2_down, grad_down * clip_factor)
    return new_up, new_down


def solution(mesh):
    n_dev = mesh.shape["fsdp"]
    rows_spec = P(None, "fsdp")

    def local_step(x_saved, grad_out, x_next, w_up, w_down, gacc_up, gacc_down, master_up, master_down, mom1_up, mom1_down, mom2_up, mom2_down):
        new_up, new_down = backward_update(x_saved, grad_out, w_up, w_down, gacc_up, gacc_down, master_up, master_down, mom1_up, mom1_down, mom2_up, mom2_down, n_dev)
        up_shard = new_up[0].astype(jnp.bfloat16)
        down_shard = new_down[0].astype(jnp.bfloat16)
        hidden_state = x_next.reshape(-1, x_next.shape[2])
        for layer_idx in range(up_shard.shape[0]):
            w_layer_up = lax.all_gather(up_shard[layer_idx], "fsdp", axis=0, tiled=True)
            w_layer_down = lax.all_gather(down_shard[layer_idx], "fsdp", axis=0, tiled=True)
            pre_act = jnp.dot(hidden_state, w_layer_up, preferred_element_type=jnp.float32)
            hidden_act = gelu_fn(pre_act).astype(jnp.bfloat16)
            hidden_state = (hidden_state.astype(jnp.float32) + jnp.dot(hidden_act, w_layer_down, preferred_element_type=jnp.float32)).astype(jnp.bfloat16)
        return (hidden_state.reshape(x_next.shape), new_up[0], new_down[0], new_up[1], new_down[1], new_up[2], new_down[2])

    return jax.shard_map(local_step, mesh=mesh, in_specs=(rows_spec, P("fsdp"), P("fsdp"), P(), P(), rows_spec, rows_spec, rows_spec, rows_spec, rows_spec, rows_spec, rows_spec, rows_spec), out_specs=(P("fsdp"), rows_spec, rows_spec, rows_spec, rows_spec, rows_spec, rows_spec), check_vma=False)
```

profile of v0, /device:TPU:0, one launch (start us, length us, event | category | flops | bytes accessed | tf_op | source)
XLA Modules:
  0.0 1655.5 jit_solution(15629677809708255876)
XLA Ops:
  7.2 14.4 fusion.87
  21.6 68.9 %fusion.47 = f32[3072,6144]{1,0:T(8,128)} fusion(bf16[3072,1536]{1,0:T(8,128)(2,1)} %bitcast.125, bf16[2,1536,6144]{2,1,0:T(8,128)(2,1)} %param.16), kind=kOutput, calls=%fused_computation.59 | convolution fusion | flops 57982058496 | bytes 103809024 | tf_op jit(solution)/shard_map/dot_general | solution.py:43
  90.5 76.1 %fusion.32 = bf16[6144,1536]{1,0:T(8,128)(2,1)} fusion(bf16[3072,1536]{1,0:T(8,128)(2,1)} %bitcast.127, f32[3072,6144]{1,0:T(8,128)} %fusion.47), kind=kOutput, calls=%fused_computation.44 | convolution fusion | flops 58161364992 | bytes 103809024 | tf_op jit(solution)/shard_map/dot_general | solution.py:47
  166.6 5.1 all-to-all-start.3
  171.7 110.9 %fusion.6 = bf16[3072,6144]{1,0:T(8,128)(2,1)} fusion(f32[3072,6144]{1,0:T(8,128)} %fusion.47, bf16[3072,1536]{1,0:T(8,128)(2,1)} %bitcast.128, bf16[2,6144,1536]{2,1,0:T(8,128)(2,1)} %param.17), kind=kOutput, calls=%fused_computation.12 | convolution fusion | flops 58359545856 | bytes 141557760 | tf_op jit(solution)/shard_map/dot_general | solution.py:45
  282.6 68.3 %add_convert_fusion.2 = bf16[3072,1536]{1,0:T(8,128)(2,1)} fusion(bf16[3072,1536]{1,0:T(8,128)(2,1)} %bitcast.129, bf16[3072,6144]{1,0:T(8,128)(2,1)} %fusion.6, bf16[2,1536,6144]{2,1,0:T(8,128)(2,1)} %param.16), kind=kOutput, calls=%fused_computation.66 | convolution fusion | flops 57996214272 | bytes 75497472 | tf_op jit(solution)/shard_map/dot_general | solution.py:50
  350.8 67.4 %convolution_convert_fusion = bf16[6144,1536]{0,1:T(8,128)(2,1)} fusion(bf16[3072,6144]{1,0:T(8,128)(2,1)} %fusion.6, bf16[3072,1536]{1,0:T(8,128)(2,1)} %bitcast.126), kind=kOutput, calls=%fused_computation.46 | convolution fusion | flops 57991495680 | bytes 66060288 | tf_op jit(solution)/shard_map/dot_general | solution.py:48
  418.3 69.1 %fusion.42 = f32[3072,6144]{1,0:T(8,128)} fusion(bf16[3072,1536]{1,0:T(8,128)(2,1)} %bitcast.123, bf16[2,1536,6144]{2,1,0:T(8,128)(2,1)} %param.16), kind=kOutput, calls=%fused_computation.54 | convolution fusion | flops 57982058496 | bytes 103809024 | tf_op jit(solution)/shard_map/dot_general | solution.py:43
  487.3 5.0 all-to-all-start.1
  492.4 76.0 %fusion.33 = bf16[6144,1536]{1,0:T(8,128)(2,1)} fusion(bf16[3072,1536]{1,0:T(8,128)(2,1)} %add_convert_fusion.2, f32[3072,6144]{1,0:T(8,128)} %fusion.42), kind=kOutput, calls=%fused_computation.45 | convolution fusion | flops 58161364992 | bytes 103809024 | tf_op jit(solution)/shard_map/dot_general | solution.py:47
  568.4 131.5 %all-to-all-done.1 = bf16[8,192,6144]{2,1,0:T(8,128)(2,1)} async-done(((bf16[8,192,6144]{2,1,0:T(8,128)(2,1)}), bf16[8,192,6144]{2,1,0:T(8,128)(2,1)}, u32[]{:S(2)}, u32[]{:S(2)}) %all-to-all-start.1) | async-done | bytes 18874400 | tf_op jit(solution)/shard_map/all_to_all | solution.py:30
  704.7 110.9 %fusion.13 = bf16[3072,6144]{1,0:T(8,128)(2,1)} fusion(f32[3072,6144]{1,0:T(8,128)} %fusion.42, bf16[3072,1536]{1,0:T(8,128)(2,1)} %add_convert_fusion.2, bf16[2,6144,1536]{2,1,0:T(8,128)(2,1)} %param.17), kind=kOutput, calls=%fused_computation.19 | convolution fusion | flops 58359545856 | bytes 141557760 | tf_op jit(solution)/shard_map/dot_general | solution.py:45
  815.6 67.6 %convolution_convert_fusion.1 = bf16[6144,1536]{0,1:T(8,128)(2,1)} fusion(bf16[3072,6144]{1,0:T(8,128)(2,1)} %fusion.13, bf16[3072,1536]{1,0:T(8,128)(2,1)} %bitcast.124), kind=kOutput, calls=%fused_computation.47 | convolution fusion | flops 57991495680 | bytes 66060288 | tf_op jit(solution)/shard_map/dot_general | solution.py:48
  883.2 28.0 %all-to-all-done.2 = bf16[8,768,1536]{2,1,0:T(8,128)(2,1)} async-done(((bf16[8,768,1536]{2,1,0:T(8,128)(2,1)}), bf16[8,768,1536]{2,1,0:T(8,128)(2,1)}, u32[]{:S(2)}, u32[]{:S(2)}) %all-to-all-start.2) | async-done | bytes 18874400 | tf_op jit(solution)/shard_map/all_to_all | solution.py:30
  915.8 11.9 convert_reduce_fusion
  927.7 12.2 convert_reduce_fusion.1
  945.2 12.8 convert_reduce_fusion.2
  958.0 164.2 %all-to-all-done = bf16[8,192,6144]{2,1,0:T(8,128)(2,1)} async-done(((bf16[8,192,6144]{2,1,0:T(8,128)(2,1)}), bf16[8,192,6144]{2,1,0:T(8,128)(2,1)}, u32[]{:S(2)}, u32[]{:S(2)}) %all-to-all-start) | async-done | bytes 18874400 | tf_op jit(solution)/shard_map/all_to_all | solution.py:30
  1122.2 11.0 convert_reduce_fusion.3
  1135.4 6.5 multiply_reduce_fusion.1
  1143.3 22.2 %psum.7 = f32[]{:T(128)} all-reduce(f32[]{:T(128)S(6)} %add.83), channel_id=1, replica_groups=mesh['fsdp'=8] {'fsdp'}, use_global_device_ids=true, to_apply=%region_6.0 | all-reduce | flops 1 | bytes 8 | tf_op jit(solution)/shard_map/psum | solution.py:56
  1166.2 29.4 %fusion.83 = (bf16[2,192,6144]{2,1,0:T(8,128)(2,1)}, f32[2,192,6144]{2,1,0:T(8,128)}, f32[2,192,6144]{2,1,0:T(8,128)}, f32[2,192,6144]{2,1,0:T(8,128)}) fusion(f32[2,192,6144]{2,1,0:T(8,128)} %param.20, f32[]{:T(128)S(6)} %mul.221, f32[2,192,6144]{2,1,0:T(8,128)} %param.18, f32[1,192,6144]{2,1,0:T(8,128)} %bitcast.113, f32[1,192,6144]{2,1,0:T(8,128)} %bitcast.116, ...), kind=kLoop, calls=%fused_computation.98 | loop fusion | flops 44826624 | bytes 80216064 | tf_op jit(solution)/shard_map/convert_element_type | solution.py:68
  1195.6 5.1 fusion.88
  1200.7 29.2 %fusion.85 = (bf16[2,768,1536]{2,1,0:T(8,128)(2,1)}, f32[2,768,1536]{2,1,0:T(8,128)}, f32[2,768,1536]{2,1,0:T(8,128)}, f32[2,768,1536]{2,1,0:T(8,128)}) fusion(f32[2,768,1536]{2,1,0:T(8,128)} %param.21, f32[]{:T(128)S(6)} %mul.221, f32[2,768,1536]{2,1,0:T(8,128)} %param.19, f32[1,768,1536]{2,1,0:T(8,128)} %bitcast.110, f32[1,768,1536]{2,1,0:T(8,128)} %bitcast.112, ...), kind=kLoop, calls=%fused_computation.99 | loop fusion | flops 44826624 | bytes 80216064 | tf_op jit(solution)/shard_map/convert_element_type | solution.py:69
  1236.0 58.7 %all-gather.9.cloned.1.call-done = bf16[1,1536,6144]{2,1,0:T(8,128)(2,1)} async-done(((bf16[1,192,6144]{2,1,0:T(8,128)(2,1)}), bf16[1,1536,6144]{2,1,0:T(8,128)(2,1)}) %all-gather.9.cloned.1.call-update) | async-done | bytes 18874384 | tf_op jit(solution)/shard_map/all_gather | solution.py:72
  1294.8 81.6 %fusion.21.clone.6 = bf16[3072,6144]{1,0:T(8,128)(2,1)} fusion(bf16[3072,1536]{1,0:T(8,128)(2,1)} %bitcast.130, bf16[1,1536,6144]{2,1,0:T(8,128)(2,1)} %all-gather.9.cloned.1.call-done), kind=kOutput, calls=%fused_computation.27.clone.clone.clone.clone.clone.1 | convolution fusion | flops 58151927808 | bytes 66060288 | tf_op jit(solution)/shard_map/dot_general | solution.py:74
  1376.4 13.2 all-gather.11.cloned.1.call-done
  1389.6 69.4 %add_convert_fusion.1 = bf16[3072,1536]{1,0:T(8,128)(2,1)} fusion(bf16[3072,1536]{1,0:T(8,128)(2,1)} %bitcast.131, bf16[1,6144,1536]{2,1,0:T(8,128)(2,1)} %all-gather.11.cloned.1.call-done, bf16[3072,6144]{1,0:T(8,128)(2,1)} %fusion.21.clone.6), kind=kOutput, calls=%fused_computation.63 | convolution fusion | flops 57996214272 | bytes 75497472 | tf_op jit(solution)/shard_map/dot_general | solution.py:76
  1459.0 25.4 %all-gather.13.cloned.1.call-done = bf16[1,1536,6144]{2,1,0:T(8,128)(2,1)} async-done(((bf16[1,192,6144]{2,1,0:T(8,128)(2,1)}), bf16[1,1536,6144]{2,1,0:T(8,128)(2,1)}) %all-gather.13.cloned.1.call-update) | async-done | bytes 18874384 | tf_op jit(solution)/shard_map/all_gather | solution.py:72
  1484.4 81.7 %fusion.29.clone.6 = bf16[3072,6144]{1,0:T(8,128)(2,1)} fusion(bf16[3072,1536]{1,0:T(8,128)(2,1)} %add_convert_fusion.1, bf16[1,1536,6144]{2,1,0:T(8,128)(2,1)} %all-gather.13.cloned.1.call-done), kind=kOutput, calls=%fused_computation.35.clone.clone.clone.clone.clone.1 | convolution fusion | flops 58151927808 | bytes 66060288 | tf_op jit(solution)/shard_map/dot_general | solution.py:74
  1566.1 13.0 all-gather.15.cloned.1.call-done
  1579.1 69.4 %add_convert_fusion = bf16[3072,1536]{1,0:T(8,128)(2,1)} fusion(bf16[3072,1536]{1,0:T(8,128)(2,1)} %add_convert_fusion.1, bf16[1,6144,1536]{2,1,0:T(8,128)(2,1)} %all-gather.15.cloned.1.call-done, bf16[3072,6144]{1,0:T(8,128)(2,1)} %fusion.29.clone.6), kind=kOutput, calls=%fused_computation.62 | convolution fusion | flops 57996214272 | bytes 75497472 | tf_op jit(solution)/shard_map/dot_general | solution.py:76
  (28 shorter events, 23.1 us)
Async XLA Ops:
  166.6 320.7 %all-to-all-start.3 = ((bf16[8,768,1536]{2,1,0:T(8,128)(2,1)}), bf16[8,768,1536]{2,1,0:T(8,128)(2,1)}, u32[]{:S(2)}, u32[]{:S(2)}) async-start(bf16[8,768,1536]{2,1,0:T(8,128)(2,1)} %bitcast.122), calls=%async_computation.3 | async-start | bytes 37748736 | tf_op jit(solution)/shard_map/all_to_all | solution.py:30
  487.3 212.6 %all-to-all-start.1 = ((bf16[8,192,6144]{2,1,0:T(8,128)(2,1)}), bf16[8,192,6144]{2,1,0:T(8,128)(2,1)}, u32[]{:S(2)}, u32[]{:S(2)}) async-start(bf16[8,192,6144]{2,1,0:T(8,128)(2,1)} %bitcast.121), calls=%async_computation.1 | async-start | bytes 37748736 | tf_op jit(solution)/shard_map/all_to_all | solution.py:30
  699.9 211.3 %all-to-all-start.2 = ((bf16[8,768,1536]{2,1,0:T(8,128)(2,1)}), bf16[8,768,1536]{2,1,0:T(8,128)(2,1)}, u32[]{:S(2)}, u32[]{:S(2)}) async-start(bf16[8,768,1536]{2,1,0:T(8,128)(2,1)} %bitcast.120), calls=%async_computation.2 | async-start | bytes 37748736 | tf_op jit(solution)/shard_map/all_to_all | solution.py:30
  911.1 211.1 %all-to-all-start = ((bf16[8,192,6144]{2,1,0:T(8,128)(2,1)}), bf16[8,192,6144]{2,1,0:T(8,128)(2,1)}, u32[]{:S(2)}, u32[]{:S(2)}) async-start(bf16[8,192,6144]{2,1,0:T(8,128)(2,1)} %bitcast.119), calls=%async_computation | async-start | bytes 37748736 | tf_op jit(solution)/shard_map/all_to_all | solution.py:30
  915.8 379.0 %all-gather.9.cloned.1.call-start = ((), (), s32[]{:S(2)}) async-start(), calls=%async_computation.4 | async-start | bytes 21233664 | tf_op jit(solution)/shard_map/all_gather | solution.py:72
  915.8 26.3 %slice-start = ((s8[9437184]{0:T(1024)(128)(4,1)}), s8[4194304]{0:T(1024)(128)(4,1)S(1)}, s32[]{:S(2)}) async-start(s8[9437184]{0:T(1024)(128)(4,1)} %bitcast.117), calls=%async_computation.8 | async-start | bytes 8388608
  915.8 26.3 %slice-start.1 = ((s8[9437184]{0:T(1024)(128)(4,1)}), s8[4194304]{0:T(1024)(128)(4,1)S(1)}, s32[]{:S(2)}) async-start(s8[9437184]{0:T(1024)(128)(4,1)} %bitcast.117), calls=%async_computation.9 | async-start | bytes 8388608
  927.7 17.5 %copy-start = (f32[768,1536]{1,0:T(8,128)}, f32[768,1536]{1,0:T(8,128)S(1)}, u32[]{:S(2)}) copy-start(f32[768,1536]{1,0:T(8,128)S(1)} %convert_reduce_fusion) | copy-start | bytes 14155780
  927.7 14.4 slice-start.2
  939.9 2.2 copy-start.1
  1122.2 13.2 copy-start.2
  1133.2 2.2 copy-start.3
  1200.7 188.9 %all-gather.11.cloned.1.call-start = ((), (), s32[]{:S(2)}) async-start(), calls=%async_computation.5 | async-start | bytes 21233664 | tf_op jit(solution)/shard_map/all_gather | solution.py:73
  1234.7 249.7 %all-gather.13.cloned.1.call-start = ((), (), s32[]{:S(2)}) async-start(), calls=%async_computation.6 | async-start | bytes 21233664 | tf_op jit(solution)/shard_map/all_gather | solution.py:72
  1235.5 343.6 %all-gather.15.cloned.1.call-start = ((), (), s32[]{:S(2)}) async-start(), calls=%async_computation.7 | async-start | bytes 21233664 | tf_op jit(solution)/shard_map/all_gather | solution.py:73
Sparse Core Ops, SparseCore 0:
  1200.8 93.9 all-gather.8
  1296.6 92.9 all-gather.10
  1391.4 92.9 all-gather.12
  1486.1 92.9 all-gather.14
where the time goes:
time: 1660 us
  matrix products  1020 us (61%)
  waiting for transfers between devices  435 us (26%)
  other arithmetic  116 us (7%)
  local copies, waits for them, and re-layouts  28.7 us (2%)
  blocking collectives  22.2 us (1%)
  starting transfers between devices  19.7 us (1%)
    all_to_all x4, waiting for transfers between devices, reduce_rows(): received = lax.all_to_all(part_grad, 'fsdp', 0, 0, tiled=True)  324 us
    dot_general x2, matrix products, backward_update(): lax.dot_general(grad_cur, w_down[layer_idx], (((1,), (1,)), ((), ())), pr...  222 us
    dot_general x2, matrix products, local_step(): jnp.dot(hidden_state, w_layer_up, preferred_element_type=jnp.float32)  163 us
    dot_general x2, matrix products, backward_update(): lax.dot_general(hidden_act.astype(jnp.bfloat16), grad_cur, (((0,), (0,)),...  152 us
    dot_general x2, matrix products, local_step(): jnp.dot(hidden_act, w_layer_down, preferred_element_type=jnp.float32)  139 us
    dot_general x2, matrix products, backward_update(): pre_act = jnp.dot(x_in, w_up[layer_idx], preferred_element_type=jnp.float32)  138 us
    dot_general x2, matrix products, backward_update(): lax.dot_general(x_in, d_pre, (((0,), (0,)), ((), ())), preferred_element_...  135 us
    all_gather x2, waiting for transfers between devices, local_step(): w_layer_up = lax.all_gather(up_shard[layer_idx], 'fsdp', axis=0, tiled=True)  84.2 us
  transfers between devices with their start and end apart: 8, of which 7 were waited for; matrix products, arithmetic and copies ran while one was open for 53% of the time, Pallas kernels for 0%

commit v1 on v0

v1 whole, which is shorter than its diff:
```python
import functools
import math
import jax
import jax.numpy as jnp
from jax import lax
from jax.experimental import pallas as pl
from jax.experimental.pallas import tpu as pltpu
from jax.sharding import PartitionSpec as P

LEARN_RATE = 0.001
BETA_ONE = 0.9
BETA_TWO = 0.95
ADAM_EPS = 1e-8
WEIGHT_DECAY = 0.1
ADAM_STEP = 3
MICRO_STEPS = 2

GELU_LIN = 0.7978845608028654
GELU_CUB = GELU_LIN * 0.044715
PAIR_SWAP = [(0, 1), (1, 0), (2, 3), (3, 2), (4, 5), (5, 4), (6, 7), (7, 6)]
SAME_CORE = [[0, 2, 4, 6], [1, 3, 5, 7]]
LANES = 256
TOK = 1024
FF = 768
VMEM_BYTES = 56 * 2**20
NN = (((1,), (0,)), ((), ()))
NT = (((1,), (1,)), ((), ()))
TN = (((0,), (0,)), ((), ()))


def fdot(left, right, dims):
    return lax.dot_general(left, right, dims, preferred_element_type=jnp.float32)


def params():
    return pltpu.CompilerParams(vmem_limit_bytes=VMEM_BYTES)


def cost(flops, moved, trans=0):
    return pl.CostEstimate(flops=int(flops), bytes_accessed=int(moved), transcendentals=int(trans))


def act_dpre_kernel(core_ref, x_ref, g_ref, up_ref, down_ref, act_ref, dpre_ref):
    for start in range(0, up_ref.shape[1], LANES):
        cols = slice(start, start + LANES)
        pre = fdot(x_ref[...], up_ref[:, cols], NN)
        d_act = fdot(g_ref[...], down_ref[cols, :], NT)
        square = pre * pre
        tanh_val = jnp.tanh(pre * (GELU_LIN + GELU_CUB * square))
        cdf = 0.5 + 0.5 * tanh_val
        slope = cdf + (0.5 * pre) * (1.0 - tanh_val * tanh_val) * (GELU_LIN + 3.0 * GELU_CUB * square)
        act_ref[:, cols] = (pre * cdf).astype(jnp.bfloat16)
        dpre_ref[:, cols] = (d_act * slope).astype(jnp.bfloat16)


def act_and_dpre(core, x_all, grad, w_up, w_down, layer):
    tokens, width = grad.shape
    ff = w_up.shape[2]
    tiles = tokens // TOK
    spec = pltpu.PrefetchScalarGridSpec(
        num_scalar_prefetch=1,
        grid=(tiles, ff // FF // 2),
        in_specs=[
            pl.BlockSpec((TOK, width), lambda i, j, c: (layer * tiles + i, 0)),
            pl.BlockSpec((TOK, width), lambda i, j, c: (i, 0)),
            pl.BlockSpec((None, width, FF), lambda i, j, c: (layer, 0, 2 * j + c[0])),
            pl.BlockSpec((None, FF, width), lambda i, j, c: (layer, 2 * j + c[0], 0)),
        ],
        out_specs=[pl.BlockSpec((TOK, FF), lambda i, j, c: (i, j))] * 2,
    )
    return pl.pallas_call(
        act_dpre_kernel,
        out_shape=[jax.ShapeDtypeStruct((tokens, ff // 2), jnp.bfloat16)] * 2,
        grid_spec=spec,
        compiler_params=params(),
        cost_estimate=cost(2 * tokens * width * ff, 4 * tokens * width + 2 * tokens * ff + 6 * width * ff, tokens * ff // 2),
        name="act_dpre",
    )(core, x_all, grad, w_up, w_down)


def back_kernel(parts, final, core_ref, dpre_ref, *refs):
    w_refs, refs = refs[:parts], refs[parts:]
    out_ref = refs[-1]
    for start in range(0, out_ref.shape[1], LANES):
        cols = slice(start, start + LANES)
        total = fdot(dpre_ref[:, 0:FF], w_refs[0][cols, :], NT)
        for q in range(1, parts):
            total += fdot(dpre_ref[:, q * FF:(q + 1) * FF], w_refs[q][cols, :], NT)
        if final:
            total = refs[0][:, cols].astype(jnp.float32) + (total + refs[1][:, cols])
        out_ref[:, cols] = total.astype(out_ref.dtype)


def grad_back(core, dpre, w_up, layer, extra=()):
    tokens, half = dpre.shape
    width = w_up.shape[1]
    parts = half // FF
    col_tile = width // 2
    tile = pl.BlockSpec((TOK, col_tile), lambda i, j, c: (i, j))
    w_specs = [pl.BlockSpec((None, col_tile, FF), functools.partial(lambda q, i, j, c: (layer, j, 2 * q + c[0]), q)) for q in range(parts)]
    spec = pltpu.PrefetchScalarGridSpec(
        num_scalar_prefetch=1,
        grid=(tokens // TOK, width // col_tile),
        in_specs=[pl.BlockSpec((TOK, half), lambda i, j, c: (i, 0))] + w_specs + [tile] * len(extra),
        out_specs=tile,
    )
    return pl.pallas_call(
        functools.partial(back_kernel, parts, bool(extra)),
        out_shape=jax.ShapeDtypeStruct((tokens, width), jnp.bfloat16 if extra else jnp.float32),
        grid_spec=spec,
        compiler_params=params(),
        cost_estimate=cost(2 * tokens * half * width, 2 * tokens * half + 4 * width * half + 6 * tokens * width),
        name="grad_back",
    )(core, dpre, *([w_up] * parts), *extra)


def token_dot_kernel(left_own, right_own, left_peer, right_peer, out_ref, total):
    k = pl.program_id(2)

    @pl.when(k == 0)
    def _():
        total[...] = fdot(left_own[...], right_own[...], TN)

    @pl.when(k == 1)
    def _():
        total[...] += fdot(left_own[...], right_own[...], TN)

    @pl.when(k == 2)
    def _():
        total[...] += fdot(left_peer[...], right_peer[...], TN)

    @pl.when(k == 3)
    def _():
        out_ref[...] = (total[...] + fdot(left_peer[...], right_peer[...], TN)).astype(jnp.bfloat16)


def token_dot(left_own, right_own, left_peer, right_peer, tokens, tile, left_row=0):
    rows, cols = left_own.shape[1], right_own.shape[1]
    depth = tokens // 2
    row_tile, col_tile = tile

    def block(width, axis, first, row):
        def index(i, j, k):
            step = jnp.minimum(k, 1) if first else jnp.maximum(k - 2, 0)
            return (row + step, (i, j)[axis])
        return pl.BlockSpec((depth, width), index)

    return pl.pallas_call(
        token_dot_kernel,
        out_shape=jax.ShapeDtypeStruct((rows, cols), jnp.bfloat16),
        grid=(rows // row_tile, cols // col_tile, 4),
        in_specs=[block(row_tile, 0, True, left_row), block(col_tile, 1, True, 0), block(row_tile, 0, False, left_row), block(col_tile, 1, False, 0)],
        out_specs=pl.BlockSpec((row_tile, col_tile), lambda i, j, k: (i, j)),
        scratch_shapes=[pltpu.VMEM((row_tile, col_tile), jnp.float32)],
        compiler_params=params(),
        cost_estimate=cost(4 * tokens * rows * cols, 4 * tokens * (rows + cols) + 2 * rows * cols),
        name="token_dot",
    )(left_own, right_own, left_peer, right_peer)


def sum_kernel(recv_ref, acc_ref, grad_ref, sq_ref):
    total = recv_ref[0].astype(jnp.float32)
    for src in range(1, recv_ref.shape[0]):
        total += recv_ref[src].astype(jnp.float32)
    grad = (acc_ref[...] + total) * (1.0 / MICRO_STEPS)
    grad_ref[...] = grad
    square = jnp.sum((grad * grad).reshape(-1, 8, grad.shape[1]), axis=0)
    first = pl.program_id(0) == 0
    for axis in range(1, 2):
        first = jnp.logical_and(first, pl.program_id(axis) == 0)

    @pl.when(first)
    def _():
        sq_ref[...] = square

    @pl.when(jnp.logical_not(first))
    def _():
        sq_ref[...] += square


def summed(recv, gacc, layer, grid, recv_block, recv_index, tile, index):
    rows, cols = gacc.shape[1:]
    return pl.pallas_call(
        sum_kernel,
        out_shape=[jax.ShapeDtypeStruct((rows, cols), jnp.float32), jax.ShapeDtypeStruct((8, tile[1]), jnp.float32)],
        grid=grid,
        in_specs=[pl.BlockSpec(recv_block, recv_index), pl.BlockSpec((None,) + tile, lambda a, b: (layer,) + index(a, b))],
        out_specs=[pl.BlockSpec(tile, index), pl.BlockSpec((8, tile[1]), lambda a, b: (0, 0))],
        compiler_params=params(),
        cost_estimate=cost(8 * rows * cols, 16 * rows * cols),
        name="grad_sum",
    )(recv, gacc)


def norm_kernel(n_dev, clip_norm, part_ref, clip_ref, slots, send_sem, recv_sem):
    me = lax.axis_index("fsdp")
    barrier = pltpu.get_barrier_semaphore()
    for step in range(1, n_dev):
        pl.semaphore_signal(barrier, inc=1, device_id=(lax.rem(me + step, n_dev),), device_id_type=pl.DeviceIdType.MESH)
    pl.semaphore_wait(barrier, n_dev - 1)

    def copy_to(step):
        return pltpu.make_async_remote_copy(
            src_ref=part_ref,
            dst_ref=slots.at[step],
            send_sem=send_sem.at[step],
            recv_sem=recv_sem.at[step],
            device_id=(lax.rem(me + step, n_dev),),
            device_id_type=pl.DeviceIdType.MESH,
        )

    for step in range(1, n_dev):
        copy_to(step).start()
    for step in range(1, n_dev):
        copy_to(step).wait()
    total = part_ref[...]
    for step in range(1, n_dev):
        total = total + slots[step]
    norm = jnp.sqrt(jnp.sum(total, keepdims=True))
    clip_ref[...] = jnp.broadcast_to(jnp.minimum(1.0, clip_norm / norm), clip_ref.shape)


def clip_factor(part, n_dev, clip_norm):
    return pl.pallas_call(
        functools.partial(norm_kernel, n_dev, clip_norm),
        out_shape=jax.ShapeDtypeStruct((8, 128), jnp.float32),
        in_specs=[pl.BlockSpec(memory_space=pltpu.VMEM)],
        out_specs=pl.BlockSpec(memory_space=pltpu.VMEM),
        scratch_shapes=[pltpu.VMEM((n_dev, 8, 128), jnp.float32), pltpu.SemaphoreType.DMA((n_dev,)), pltpu.SemaphoreType.DMA((n_dev,))],
        compiler_params=pltpu.CompilerParams(collective_id=0, has_side_effects=True),
        name="clip_norm",
    )(part)


def adamw_kernel(aliased, clip_ref, grad_ref, master_ref, one_ref, two_ref, *refs):
    new_master_ref, new_one_ref, new_two_ref, weight_ref = refs[aliased:]
    grad = grad_ref[...] * clip_ref[0:1, 0:1]
    master = master_ref[...]
    one = BETA_ONE * one_ref[...] + (1.0 - BETA_ONE) * grad
    two = BETA_TWO * two_ref[...] + (1.0 - BETA_TWO) * grad * grad
    first_hat = one / (1.0 - BETA_ONE ** ADAM_STEP)
    second_hat = two / (1.0 - BETA_TWO ** ADAM_STEP)
    master = master - LEARN_RATE * (first_hat / (jnp.sqrt(second_hat) + ADAM_EPS) + WEIGHT_DECAY * master)
    new_one_ref[...] = one
    new_two_ref[...] = two
    new_master_ref[...] = master
    weight_ref[...] = master.astype(jnp.bfloat16)


def adamw(clip, grad, master, mom_one, mom_two, layer, tile, earlier=()):
    rows, cols = grad.shape
    index = lambda a, b: (a, b)
    whole = pl.BlockSpec((None,) + tile, lambda a, b: (layer, a, b))
    part = pl.BlockSpec(tile, index)
    full = jax.ShapeDtypeStruct(master.shape, jnp.float32)
    return pl.pallas_call(
        functools.partial(adamw_kernel, len(earlier)),
        out_shape=[full] * 3 + [jax.ShapeDtypeStruct((rows, cols), jnp.bfloat16)],
        grid=(rows // tile[0], cols // tile[1]),
        in_specs=[pl.BlockSpec((8, 128), lambda a, b: (0, 0)), part, whole, whole, whole] + [pl.BlockSpec(memory_space=pl.ANY)] * len(earlier),
        out_specs=[whole] * 3 + [part],
        input_output_aliases={5 + i: i for i in range(len(earlier))},
        compiler_params=params(),
        cost_estimate=cost(20 * rows * cols, 30 * rows * cols, 2 * rows * cols),
        name="adamw",
    )(clip, grad, master, mom_one, mom_two, *earlier)


def up_kernel(x_ref, w_ref, act_ref):
    for start in range(0, w_ref.shape[1], LANES):
        cols = slice(start, start + LANES)
        pre = fdot(x_ref[...], w_ref[:, cols], NN)
        cdf = 0.5 + 0.5 * jnp.tanh(pre * (GELU_LIN + GELU_CUB * (pre * pre)))
        act_ref[:, cols] = (pre * cdf).astype(jnp.bfloat16)


def forward_up(hidden, weight):
    tokens, width = hidden.shape
    ff = weight.shape[1]
    return pl.pallas_call(
        up_kernel,
        out_shape=jax.ShapeDtypeStruct((tokens, ff), jnp.bfloat16),
        grid=(tokens // TOK, ff // FF),
        in_specs=[pl.BlockSpec((TOK, width), lambda i, j: (i, 0)), pl.BlockSpec((width, FF), lambda i, j: (0, j))],
        out_specs=pl.BlockSpec((TOK, FF), lambda i, j: (i, j)),
        compiler_params=params(),
        cost_estimate=cost(2 * tokens * width * ff, 2 * tokens * width + 2 * tokens * ff + 2 * width * ff, tokens * ff),
        name="forward_up",
    )(hidden, weight)


def down_kernel(act_ref, w_ref, hidden_ref, out_ref, total):
    k = pl.program_id(2)
    last = pl.num_programs(2) - 1

    @pl.when(k == 0)
    def _():
        total[...] = fdot(act_ref[...], w_ref[...], NN)

    @pl.when(jnp.logical_and(k > 0, k < last))
    def _():
        total[...] += fdot(act_ref[...], w_ref[...], NN)

    @pl.when(k == last)
    def _():
        out_ref[...] = (hidden_ref[...].astype(jnp.float32) + (total[...] + fdot(act_ref[...], w_ref[...], NN))).astype(jnp.bfloat16)


def forward_down(act, weight, hidden):
    tokens, ff = act.shape
    width = weight.shape[1]
    col_tile, depth = width // 2, 2 * FF
    tile = pl.BlockSpec((TOK, col_tile), lambda i, j, k: (i, j))
    return pl.pallas_call(
        down_kernel,
        out_shape=jax.ShapeDtypeStruct((tokens, width), jnp.bfloat16),
        grid=(tokens // TOK, width // col_tile, ff // depth),
        in_specs=[pl.BlockSpec((TOK, depth), lambda i, j, k: (i, k)), pl.BlockSpec((depth, col_tile), lambda i, j, k: (k, j)), tile],
        out_specs=tile,
        scratch_shapes=[pltpu.VMEM((TOK, col_tile), jnp.float32)],
        compiler_params=params(),
        cost_estimate=cost(2 * tokens * width * ff, 2 * tokens * ff + 4 * tokens * width + 2 * width * ff),
        name="forward_down",
    )(act, weight, hidden)


def pair_swap(value):
    return lax.ppermute(value, "fsdp", PAIR_SWAP)


def after(value, *first):
    return lax.optimization_barrier((value,) + first)[0]


def gradient_rows(x_saved, grad_out, w_up, w_down, gacc_up, gacc_down):
    layers, width, ff = w_up.shape
    core = lax.rem(lax.axis_index("fsdp"), 2).reshape(1)
    x_own = x_saved.reshape(-1, width)
    grad_own = grad_out.reshape(-1, width)
    tokens = grad_own.shape[0]
    x_peer, grad_peer = pair_swap(x_own), pair_swap(grad_own)
    rows_up, rows_down = [None] * layers, [None] * layers
    recv_down = None
    for layer in range(layers - 1, -1, -1):
        act_own, dpre_own = act_and_dpre(core, x_own, grad_own, w_up, w_down, layer)
        peer_core = after(core, act_own) if recv_down is None else after(core, act_own, recv_down)
        act_peer, dpre_peer = act_and_dpre(peer_core, x_peer, grad_peer, w_up, w_down, layer)
        old_grads = (grad_own, grad_peer)
        if layer > 0:
            from_peer = pair_swap(grad_back(core, dpre_peer, w_up, layer))
            grad_own = grad_back(core, dpre_own, w_up, layer, (grad_own, from_peer))
            grad_peer = pair_swap(grad_own)
        part_down = token_dot(act_own, old_grads[0], act_peer, old_grads[1], tokens, (TOK, FF))
        recv_down = lax.all_to_all(part_down, "fsdp", 0, 0, tiled=True, axis_index_groups=SAME_CORE)
        part_up = token_dot(x_own, dpre_own, x_peer, dpre_peer, tokens, (FF, TOK), layer * 2)
        recv_up = lax.all_to_all(part_up, "fsdp", 0, 0, tiled=True)
        rows_down[layer] = summed(recv_down.reshape(4, -1, width), gacc_down, layer, (4, 1), (4, 192, width), lambda a, b: (0, a, 0), (192, width), lambda a, b: (a, 0))
        rows_up[layer] = summed(recv_up.reshape(4, 2, -1, ff // 2), gacc_up, layer, (4, 2), (4, None, 192, FF), lambda a, b: (0, b, 0, a), (192, FF), lambda a, b: (0, 2 * a + b))
    return rows_up, rows_down


def solution(mesh):
    n_dev = mesh.shape["fsdp"]
    rows_spec = P(None, "fsdp")

    def local_step(x_saved, grad_out, x_next, w_up, w_down, gacc_up, gacc_down, master_up, master_down, mom1_up, mom1_down, mom2_up, mom2_down):
        layers, width, ff = w_up.shape
        clip_norm = 0.1 * math.sqrt(2 * layers * width * ff)
        rows_up, rows_down = gradient_rows(x_saved, grad_out, w_up, w_down, gacc_up, gacc_down)
        part = sum(jnp.sum(sq.reshape(8, -1, 128), axis=1) for _, sq in rows_up + rows_down)
        clip = clip_factor(part, n_dev, clip_norm)
        new_up, new_down = (), ()
        up_shards, down_shards = [], []
        for layer in range(layers):
            *new_up, shard = adamw(clip, rows_up[layer][0], master_up, mom1_up, mom2_up, layer, (192, FF), new_up)
            up_shards.append(shard)
            *new_down, shard = adamw(clip, rows_down[layer][0], master_down, mom1_down, mom2_down, layer, (96, width), new_down)
            down_shards.append(shard)
        hidden = x_next.reshape(-1, width)
        for layer in range(layers):
            act = forward_up(hidden, lax.all_gather(up_shards[layer], "fsdp", axis=0, tiled=True))
            hidden = forward_down(act, lax.all_gather(down_shards[layer], "fsdp", axis=0, tiled=True), hidden)
        return (hidden.reshape(x_next.shape), new_up[0], new_down[0], new_up[1], new_down[1], new_up[2], new_down[2])

    return jax.shard_map(local_step, mesh=mesh, in_specs=(rows_spec, P("fsdp"), P("fsdp"), P(), P(), rows_spec, rows_spec, rows_spec, rows_spec, rows_spec, rows_spec, rows_spec, rows_spec), out_specs=(P("fsdp"), rows_spec, rows_spec, rows_spec, rows_spec, rows_spec, rows_spec), check_vma=False)
```

time: 1660 us -> 1370 us (0.83)
  Pallas kernels: 0 us -> 1110 us
  matrix products: 1020 us -> 0 us
  waiting for transfers between devices: 435 us -> 211 us
  other arithmetic: 116 us -> 2.16 us
  local copies, waits for them, and re-layouts: 28.7 us -> 0.01 us
  blocking collectives: 22.2 us -> 0 us
    pallas_call x0 -> x23, Pallas kernels: none -> 1110 us  [the longest x4 328 us: token_dot(): pl.pallas_call(token_dot_kernel, out_shape=jax.ShapeDtypeStruct((rows, co...]
    dot_general x13 -> x0, matrix products: 1020 us -> none  [the longest x2 222 us: backward_update(): lax.dot_general(grad_cur, w_down[layer_idx], (((1,), (1,)), ((), ())), pr...]
    all_to_all x4, waiting for transfers between devices: 324 us -> 103 us  [the longest x2 79.1 us: gradient_rows(): recv_up = lax.all_to_all(part_up, 'fsdp', 0, 0, tiled=True)]
    convert_element_type x2 -> x0, other arithmetic: 58.6 us -> none  [the longest x1 29.4 us: local_step(): up_shard = new_up[0].astype(jnp.bfloat16)]
    reduce_sum x6 -> x2, other arithmetic: 57.4 us -> 1.56 us  [local_step(): jnp.sum(sq.reshape(8, -1, 128), axis=1)]
    slice x3 -> x0, local copies, waits for them, and re-layouts: 24.3 us -> none  [the longest x1 14.4 us: backward_update(): x_in = x_tokens[layer_idx]]
    psum x1 -> x0, blocking collectives: 22.2 us -> none  [backward_update(): lax.psum(local_sq, 'fsdp')]
  transfers between devices with their start and end apart: 8 -> 12, of which waited for: 7 -> 6; matrix products, arithmetic and copies ran while one was open for 53% -> 0% of each run, Pallas kernels for 0% -> 66%
where the time goes in v1:
time: 1370 us; the launch traced here: 1360 us
  Pallas kernels  1110 us (81%)
  waiting for transfers between devices  211 us (15%)
  starting transfers between devices  21.4 us (2%)
  between operations  14.3 us (1%)
    pallas_call x4, Pallas kernels, token_dot(): pl.pallas_call(token_dot_kernel, out_shape=jax.ShapeDtypeStruct((rows, co...  328 us
    pallas_call x4, Pallas kernels, act_and_dpre(): pl.pallas_call(act_dpre_kernel, out_shape=[jax.ShapeDtypeStruct((tokens,...  312 us
    pallas_call x2, Pallas kernels, forward_up(): pl.pallas_call(up_kernel, out_shape=jax.ShapeDtypeStruct((tokens, ff), jn...  150 us
    pallas_call x2, Pallas kernels, forward_down(): pl.pallas_call(down_kernel, out_shape=jax.ShapeDtypeStruct((tokens, width...  142 us
    all_to_all x2, waiting for transfers between devices, gradient_rows(): recv_up = lax.all_to_all(part_up, 'fsdp', 0, 0, tiled=True)  79.1 us
    pallas_call x2, Pallas kernels, grad_back(): pl.pallas_call(functools.partial(back_kernel, parts, bool(extra)), out_sh...  75.9 us
    all_gather x2, waiting for transfers between devices, local_step(): lax.all_gather(up_shards[layer], 'fsdp', axis=0, tiled=True)  68.6 us
    pallas_call x4, Pallas kernels, adamw(): pl.pallas_call(functools.partial(adamw_kernel, len(earlier)), out_shape=[...  62.7 us
  transfers between devices with their start and end apart: 12, of which 6 were waited for; matrix products, arithmetic and copies ran while one was open for 0% of the time, Pallas kernels for 66%

profile of v1, /device:TPU:0, one launch (start us, length us, event | category | flops | bytes accessed | tf_op | source)
XLA Modules:
  0.0 1361.4 jit_solution(1779136151598310573)
XLA Ops:
  8.1 78.2 %act_dpre.4 = (bf16[3072,3072]{1,0:T(8,128)(2,1)}, bf16[3072,3072]{1,0:T(8,128)(2,1)}) custom-call(s32[1]{0:T(128)} %bitcast.2.core_ref, bf16[6144,1536]{1,0:T(8,128)(2,1)} %bitcast.28, bf16[3072,1536]{1,0:T(8,128)(2,1)} %bitcast.20, bf16[2,1536,6144]{2,1,0:T(8,128)(2,1)} %up_ref.7, bf16[2,6144,1536]{2,1,0:T(8,128)(2,1)} %down_ref.7), custom_call_target="tpu_custom_call" | custom-call | flops 57982058496 | bytes 113246208 | tf_op jit(solution)/shard_map/act_dpre/pallas_call | solution.py:71
  86.3 78.1 %act_dpre.5 = (bf16[3072,3072]{1,0:T(8,128)(2,1)}, bf16[3072,3072]{1,0:T(8,128)(2,1)}) custom-call(s32[1]{0:T(128)} %bitcast.2.core_ref, bf16[6144,1536]{1,0:T(8,128)(2,1)} %collective-permute-done.x_ref.left_peer, bf16[3072,1536]{1,0:T(8,128)(2,1)} %collective-permute-done.1.g_ref.right_peer, bf16[2,1536,6144]{2,1,0:T(8,128)(2,1)} %up_ref.7, ...), custom_call_target="tpu_custom_call" | custom-call | flops 57982058496 | bytes 113246208 | tf_op jit(solution)/shard_map/act_dpre/pallas_call | solution.py:71
  164.3 36.7 %grad_back.2 = f32[3072,1536]{1,0:T(8,128)} custom-call(s32[1]{0:T(128)} %bitcast.2.core_ref, bf16[3072,3072]{1,0:T(8,128)(2,1)} %get-tuple-element.44.dpre_ref.right_peer, bf16[2,1536,6144]{2,1,0:T(8,128)(2,1)} %up_ref.7, bf16[2,1536,6144]{2,1,0:T(8,128)(2,1)} %up_ref.7, bf16[2,1536,6144]{2,1,0:T(8,128)(2,1)} %up_ref.7, bf16[2,1536,6144]{2,1,0:T(8,128)(2,1)} %up_ref.7), custom_call_target="tpu_custom_call" | custom-call | flops 28991029248 | bytes 66060288 | tf_op jit(solution)/shard_map/grad_back/pallas_call | solution.py:107
  201.5 83.1 %token_dot.7 = bf16[3072,1536]{1,0:T(8,128)(2,1)} custom-call(bf16[3072,3072]{1,0:T(8,128)(2,1)} %get-tuple-element.42.left_own, bf16[3072,1536]{1,0:T(8,128)(2,1)} %bitcast.21, bf16[3072,3072]{1,0:T(8,128)(2,1)} %get-tuple-element.53.left_peer, bf16[3072,1536]{1,0:T(8,128)(2,1)} %collective-permute-done.1.g_ref.right_peer), custom_call_target="tpu_custom_call" | custom-call | flops 57982058496 | bytes 66060288 | tf_op jit(solution)/shard_map/token_dot/pallas_call | solution.py:148
  284.6 6.0 all-to-all-start.3
  290.6 39.2 %grad_back.3.g_ref.right_own = bf16[3072,1536]{1,0:T(8,128)(2,1)} custom-call(s32[1]{0:T(128)} %bitcast.2.core_ref, bf16[3072,3072]{1,0:T(8,128)(2,1)} %get-tuple-element.41.dpre_ref.right_own, bf16[2,1536,6144]{2,1,0:T(8,128)(2,1)} %up_ref.7, bf16[2,1536,6144]{2,1,0:T(8,128)(2,1)} %up_ref.7, bf16[2,1536,6144]{2,1,0:T(8,128)(2,1)} %up_ref.7, ...), custom_call_target="tpu_custom_call" | custom-call | flops 28991029248 | bytes 66060288 | tf_op jit(solution)/shard_map/grad_back/pallas_call | solution.py:107
  329.8 81.0 %token_dot.5 = bf16[1536,3072]{1,0:T(8,128)(2,1)} custom-call(bf16[6144,1536]{1,0:T(8,128)(2,1)} %bitcast.29, bf16[3072,3072]{1,0:T(8,128)(2,1)} %get-tuple-element.41.dpre_ref.right_own, bf16[6144,1536]{1,0:T(8,128)(2,1)} %collective-permute-done.x_ref.left_peer, bf16[3072,3072]{1,0:T(8,128)(2,1)} %get-tuple-element.44.dpre_ref.right_peer), custom_call_target="tpu_custom_call" | custom-call | flops 57982058496 | bytes 66060288 | tf_op jit(solution)/shard_map/token_dot/pallas_call | solution.py:148
  410.8 78.2 %act_dpre.6 = (bf16[3072,3072]{1,0:T(8,128)(2,1)}, bf16[3072,3072]{1,0:T(8,128)(2,1)}) custom-call(s32[1]{0:T(128)} %bitcast.2.core_ref, bf16[6144,1536]{1,0:T(8,128)(2,1)} %bitcast.30, bf16[3072,1536]{1,0:T(8,128)(2,1)} %grad_back.3.g_ref.right_own, bf16[2,1536,6144]{2,1,0:T(8,128)(2,1)} %up_ref.7, bf16[2,6144,1536]{2,1,0:T(8,128)(2,1)} %down_ref.7), custom_call_target="tpu_custom_call" | custom-call | flops 57982058496 | bytes 113246208 | tf_op jit(solution)/shard_map/act_dpre/pallas_call | solution.py:71
  489.0 3.9 all-to-all-start.1
  492.9 77.9 %act_dpre.7 = (bf16[3072,3072]{1,0:T(8,128)(2,1)}, bf16[3072,3072]{1,0:T(8,128)(2,1)}) custom-call(s32[1]{0:T(128)} %bitcast.2.core_ref, bf16[6144,1536]{1,0:T(8,128)(2,1)} %collective-permute-done.x_ref.left_peer, bf16[3072,1536]{1,0:T(8,128)(2,1)} %collective-permute-done.3.g_ref.right_peer, bf16[2,1536,6144]{2,1,0:T(8,128)(2,1)} %up_ref.7, ...), custom_call_target="tpu_custom_call" | custom-call | flops 57982058496 | bytes 113246208 | tf_op jit(solution)/shard_map/act_dpre/pallas_call | solution.py:71
  570.8 83.1 %token_dot.6 = bf16[3072,1536]{1,0:T(8,128)(2,1)} custom-call(bf16[3072,3072]{1,0:T(8,128)(2,1)} %get-tuple-element.46.left_own, bf16[3072,1536]{1,0:T(8,128)(2,1)} %grad_back.3.g_ref.right_own, bf16[3072,3072]{1,0:T(8,128)(2,1)} %get-tuple-element.51.left_peer, bf16[3072,1536]{1,0:T(8,128)(2,1)} %collective-permute-done.3.g_ref.right_peer), custom_call_target="tpu_custom_call" | custom-call | flops 57982058496 | bytes 66060288 | tf_op jit(solution)/shard_map/token_dot/pallas_call | solution.py:148
  653.9 5.9 all-to-all-start.2
  659.9 81.1 %token_dot.4 = bf16[1536,3072]{1,0:T(8,128)(2,1)} custom-call(bf16[6144,1536]{1,0:T(8,128)(2,1)} %bitcast.31, bf16[3072,3072]{1,0:T(8,128)(2,1)} %get-tuple-element.45.right_own, bf16[6144,1536]{1,0:T(8,128)(2,1)} %collective-permute-done.x_ref.left_peer, bf16[3072,3072]{1,0:T(8,128)(2,1)} %get-tuple-element.48.right_peer), custom_call_target="tpu_custom_call" | custom-call | flops 57982058496 | bytes 66060288 | tf_op jit(solution)/shard_map/token_dot/pallas_call | solution.py:148
  740.9 24.0 %all-to-all-done.2.recv_ref = bf16[4,768,1536]{2,1,0:T(8,128)(2,1)} async-done(((bf16[4,768,1536]{2,1,0:T(8,128)(2,1)}), bf16[4,768,1536]{2,1,0:T(8,128)(2,1)}, u32[]{:S(2)}, u32[]{:S(2)}) %all-to-all-start.2) | async-done | bytes 9437216 | tf_op jit(solution)/shard_map/all_to_all | solution.py:354
  768.7 7.8 grad_sum.7
  776.5 9.6 grad_sum.5
  786.1 7.9 grad_sum.6
  794.8 79.1 %all-to-all-done = bf16[8,192,3072]{2,1,0:T(8,128)(2,1)} async-done(((bf16[8,192,3072]{2,1,0:T(8,128)(2,1)}), bf16[8,192,3072]{2,1,0:T(8,128)(2,1)}, u32[]{:S(2)}, u32[]{:S(2)}) %all-to-all-start) | async-done | bytes 9437216 | tf_op jit(solution)/shard_map/all_to_all | solution.py:356
  873.9 9.5 grad_sum.4
  884.8 6.1 clip_norm.1.clip_ref
  890.9 15.7 %adamw.4 = (f32[2,192,6144]{2,1,0:T(8,128)}, f32[2,192,6144]{2,1,0:T(8,128)}, f32[2,192,6144]{2,1,0:T(8,128)}, bf16[192,6144]{1,0:T(8,128)(2,1)}) custom-call(f32[8,128]{1,0:T(8,128)} %clip_norm.1.clip_ref, f32[192,6144]{1,0:T(8,128)} %get-tuple-element.55.grad_ref, f32[2,192,6144]{2,1,0:T(8,128)} %master_ref.6, f32[2,192,6144]{2,1,0:T(8,128)} %one_ref.6, ...), custom_call_target="tpu_custom_call" | custom-call | flops 23592960 | bytes 35389440 | tf_op jit(solution)/shard_map/adamw/pallas_call | solution.py:256
  906.6 15.7 %adamw.5 = (f32[2,768,1536]{2,1,0:T(8,128)}, f32[2,768,1536]{2,1,0:T(8,128)}, f32[2,768,1536]{2,1,0:T(8,128)}, bf16[768,1536]{1,0:T(8,128)(2,1)}) custom-call(f32[8,128]{1,0:T(8,128)} %clip_norm.1.clip_ref, f32[768,1536]{1,0:T(8,128)} %get-tuple-element.57.grad_ref, f32[2,768,1536]{2,1,0:T(8,128)} %master_ref.7, f32[2,768,1536]{2,1,0:T(8,128)} %one_ref.7, ...), custom_call_target="tpu_custom_call" | custom-call | flops 23592960 | bytes 35389440 | tf_op jit(solution)/shard_map/adamw/pallas_call | solution.py:256
  922.4 15.7 %adamw.6 = (f32[2,192,6144]{2,1,0:T(8,128)}, f32[2,192,6144]{2,1,0:T(8,128)}, f32[2,192,6144]{2,1,0:T(8,128)}, bf16[192,6144]{1,0:T(8,128)(2,1)}) custom-call(f32[8,128]{1,0:T(8,128)} %clip_norm.1.clip_ref, f32[192,6144]{1,0:T(8,128)} %get-tuple-element.59.grad_ref, ...), custom_call_target="tpu_custom_call", output_to_operand_aliasing={{0}: (5, {}), {1}: (6, {}), {2}: (7, {})} | custom-call | flops 23592960 | bytes 35389440 | tf_op jit(solution)/shard_map/adamw/pallas_call | solution.py:256
  938.4 15.6 %adamw.7 = (f32[2,768,1536]{2,1,0:T(8,128)}, f32[2,768,1536]{2,1,0:T(8,128)}, f32[2,768,1536]{2,1,0:T(8,128)}, bf16[768,1536]{1,0:T(8,128)(2,1)}) custom-call(f32[8,128]{1,0:T(8,128)} %clip_norm.1.clip_ref, f32[768,1536]{1,0:T(8,128)} %get-tuple-element.64.grad_ref, ...), custom_call_target="tpu_custom_call", output_to_operand_aliasing={{0}: (5, {}), {1}: (6, {}), {2}: (7, {})} | custom-call | flops 23592960 | bytes 35389440 | tf_op jit(solution)/shard_map/adamw/pallas_call | solution.py:256
  954.0 44.8 %all-gather.5.cloned.1.call-done.w_ref = bf16[1536,6144]{1,0:T(8,128)(2,1)} async-done(((bf16[192,6144]{1,0:T(8,128)(2,1)}), bf16[1536,6144]{1,0:T(8,128)(2,1)}) %all-gather.5.cloned.1.call-update) | async-done | bytes 18874384 | tf_op jit(solution)/shard_map/all_gather | solution.py:381
  998.9 75.2 %forward_up.2.act_ref = bf16[3072,6144]{1,0:T(8,128)(2,1)} custom-call(bf16[3072,1536]{1,0:T(8,128)(2,1)} %bitcast.32, bf16[1536,6144]{1,0:T(8,128)(2,1)} %all-gather.5.cloned.1.call-done.w_ref), custom_call_target="tpu_custom_call" | custom-call | flops 57982058496 | bytes 66060288 | tf_op jit(solution)/shard_map/forward_up/pallas_call | solution.py:280
  1074.0 19.6 %all-gather.7.cloned.1.call-done.w_ref = bf16[6144,1536]{1,0:T(8,128)(2,1)} async-done(((bf16[768,1536]{1,0:T(8,128)(2,1)}), bf16[6144,1536]{1,0:T(8,128)(2,1)}) %all-gather.7.cloned.1.call-update) | async-done | bytes 18874384 | tf_op jit(solution)/shard_map/all_gather | solution.py:382
  1093.7 71.1 %forward_down.2.x_ref.hidden_ref = bf16[3072,1536]{1,0:T(8,128)(2,1)} custom-call(bf16[3072,6144]{1,0:T(8,128)(2,1)} %forward_up.2.act_ref, bf16[6144,1536]{1,0:T(8,128)(2,1)} %all-gather.7.cloned.1.call-done.w_ref, bf16[3072,1536]{1,0:T(8,128)(2,1)} %bitcast.33), custom_call_target="tpu_custom_call" | custom-call | flops 57982058496 | bytes 75497472 | tf_op jit(solution)/shard_map/forward_down/pallas_call | solution.py:314
  1164.7 23.8 %all-gather.9.cloned.1.call-done.w_ref = bf16[1536,6144]{1,0:T(8,128)(2,1)} async-done(((bf16[192,6144]{1,0:T(8,128)(2,1)}), bf16[1536,6144]{1,0:T(8,128)(2,1)}) %all-gather.9.cloned.1.call-update) | async-done | bytes 18874384 | tf_op jit(solution)/shard_map/all_gather | solution.py:381
  1188.5 75.2 %forward_up.3.act_ref = bf16[3072,6144]{1,0:T(8,128)(2,1)} custom-call(bf16[3072,1536]{1,0:T(8,128)(2,1)} %forward_down.2.x_ref.hidden_ref, bf16[1536,6144]{1,0:T(8,128)(2,1)} %all-gather.9.cloned.1.call-done.w_ref), custom_call_target="tpu_custom_call" | custom-call | flops 57982058496 | bytes 66060288 | tf_op jit(solution)/shard_map/forward_up/pallas_call | solution.py:280
  1263.6 19.5 %all-gather.11.cloned.1.call-done.w_ref = bf16[6144,1536]{1,0:T(8,128)(2,1)} async-done(((bf16[768,1536]{1,0:T(8,128)(2,1)}), bf16[6144,1536]{1,0:T(8,128)(2,1)}) %all-gather.11.cloned.1.call-update) | async-done | bytes 18874384 | tf_op jit(solution)/shard_map/all_gather | solution.py:382
  1283.1 71.3 %forward_down.3 = bf16[3072,1536]{1,0:T(8,128)(2,1)} custom-call(bf16[3072,6144]{1,0:T(8,128)(2,1)} %forward_up.3.act_ref, bf16[6144,1536]{1,0:T(8,128)(2,1)} %all-gather.11.cloned.1.call-done.w_ref, bf16[3072,1536]{1,0:T(8,128)(2,1)} %forward_down.2.x_ref.hidden_ref), custom_call_target="tpu_custom_call" | custom-call | flops 57982058496 | bytes 75497472 | tf_op jit(solution)/shard_map/forward_down/pallas_call | solution.py:314
  (26 shorter events, 7.8 us)
Async XLA Ops:
  7.2 79.1 %collective-permute-start = (bf16[6144,1536]{1,0:T(8,128)(2,1)}, bf16[6144,1536]{1,0:T(8,128)(2,1)}, u32[]{:S(2)}, u32[]{:S(2)}) collective-permute-start(bf16[6144,1536]{1,0:T(8,128)(2,1)} %bitcast.27), channel_id=1, source_target_pairs={{0,1},{1,0},{2,3},{3,2},{4,5},{5,4},{6,7},{7,6}} | collective-permute-start | bytes 56623112 | tf_op jit(solution)/shard_map/ppermute | solution.py:328
  8.0 78.2 %collective-permute-start.1 = (bf16[3072,1536]{1,0:T(8,128)(2,1)}, bf16[3072,1536]{1,0:T(8,128)(2,1)}, u32[]{:S(2)}, u32[]{:S(2)}) collective-permute-start(bf16[3072,1536]{1,0:T(8,128)(2,1)} %bitcast.19), channel_id=1, source_target_pairs={{0,1},{1,0},{2,3},{3,2},{4,5},{5,4},{6,7},{7,6}} | collective-permute-start | bytes 28311560 | tf_op jit(solution)/shard_map/ppermute | solution.py:328
  201.0 89.6 %collective-permute-start.2 = (f32[3072,1536]{1,0:T(8,128)}, f32[3072,1536]{1,0:T(8,128)}, u32[]{:S(2)}, u32[]{:S(2)}) collective-permute-start(f32[3072,1536]{1,0:T(8,128)} %grad_back.2), channel_id=1, source_target_pairs={{0,1},{1,0},{2,3},{3,2},{4,5},{5,4},{6,7},{7,6}} | collective-permute-start | bytes 56623112 | tf_op jit(solution)/shard_map/ppermute | solution.py:328
  284.6 204.4 %all-to-all-start.3 = ((bf16[4,768,1536]{2,1,0:T(8,128)(2,1)}), bf16[4,768,1536]{2,1,0:T(8,128)(2,1)}, u32[]{:S(2)}, u32[]{:S(2)}) async-start(bf16[4,768,1536]{2,1,0:T(8,128)(2,1)} %bitcast.25), calls=%async_computation.3 | async-start | bytes 18874368 | tf_op jit(solution)/shard_map/all_to_all | solution.py:354
  329.8 163.1 %collective-permute-start.3 = (bf16[3072,1536]{1,0:T(8,128)(2,1)}, bf16[3072,1536]{1,0:T(8,128)(2,1)}, u32[]{:S(2)}, u32[]{:S(2)}) collective-permute-start(bf16[3072,1536]{1,0:T(8,128)(2,1)} %grad_back.3.g_ref.right_own), channel_id=1, source_target_pairs={{0,1},{1,0},{2,3},{3,2},{4,5},{5,4},{6,7},{7,6}} | collective-permute-start | bytes 28311560 | tf_op jit(solution)/shard_map/ppermute | solution.py:328
  489.0 164.9 %all-to-all-start.1 = ((bf16[8,192,3072]{2,1,0:T(8,128)(2,1)}), bf16[8,192,3072]{2,1,0:T(8,128)(2,1)}, u32[]{:S(2)}, u32[]{:S(2)}) async-start(bf16[8,192,3072]{2,1,0:T(8,128)(2,1)} %bitcast.24), calls=%async_computation.1 | async-start | bytes 18874368 | tf_op jit(solution)/shard_map/all_to_all | solution.py:356
  653.9 111.0 %all-to-all-start.2 = ((bf16[4,768,1536]{2,1,0:T(8,128)(2,1)}), bf16[4,768,1536]{2,1,0:T(8,128)(2,1)}, u32[]{:S(2)}, u32[]{:S(2)}) async-start(bf16[4,768,1536]{2,1,0:T(8,128)(2,1)} %bitcast.26), calls=%async_computation.2 | async-start | bytes 18874368 | tf_op jit(solution)/shard_map/all_to_all | solution.py:354
  764.9 109.0 %all-to-all-start = ((bf16[8,192,3072]{2,1,0:T(8,128)(2,1)}), bf16[8,192,3072]{2,1,0:T(8,128)(2,1)}, u32[]{:S(2)}, u32[]{:S(2)}) async-start(bf16[8,192,3072]{2,1,0:T(8,128)(2,1)} %bitcast.23), calls=%async_computation | async-start | bytes 18874368 | tf_op jit(solution)/shard_map/all_to_all | solution.py:356
  768.7 230.2 %all-gather.5.cloned.1.call-start = ((), (), s32[]{:S(2)}) async-start(), calls=%async_computation.4 | async-start | bytes 21233664 | tf_op jit(solution)/shard_map/all_gather | solution.py:381
  786.1 7.9 copy-start
  873.9 9.5 copy-start.1
  906.6 187.1 %all-gather.7.cloned.1.call-start = ((), (), s32[]{:S(2)}) async-start(), calls=%async_computation.5 | async-start | bytes 21233664 | tf_op jit(solution)/shard_map/all_gather | solution.py:382
  922.4 266.1 %all-gather.9.cloned.1.call-start = ((), (), s32[]{:S(2)}) async-start(), calls=%async_computation.6 | async-start | bytes 21233664 | tf_op jit(solution)/shard_map/all_gather | solution.py:381
  938.1 345.0 %all-gather.11.cloned.1.call-start = ((), (), s32[]{:S(2)}) async-start(), calls=%async_computation.7 | async-start | bytes 21233664 | tf_op jit(solution)/shard_map/all_gather | solution.py:382
Sparse Core Ops, SparseCore 0:
  906.7 92.1 all-gather.4
  1000.7 92.9 all-gather.6
  1095.5 92.9 all-gather.8
  1190.1 92.9 all-gather.10

commit v2 on v1

--- a/solution.py
+++ b/solution.py
@@ -21,7 +21,10 @@
 SAME_CORE = [[0, 2, 4, 6], [1, 3, 5, 7]]
 LANES = 256
 TOK = 1024
+SUB = 256
 FF = 768
+DEPTH = 768
+WIDE = 1536
 VMEM_BYTES = 56 * 2**20
 NN = (((1,), (0,)), ((), ()))
 NT = (((1,), (1,)), ((), ()))
@@ -43,14 +46,16 @@
 def act_dpre_kernel(core_ref, x_ref, g_ref, up_ref, down_ref, act_ref, dpre_ref):
     for start in range(0, up_ref.shape[1], LANES):
         cols = slice(start, start + LANES)
-        pre = fdot(x_ref[...], up_ref[:, cols], NN)
-        d_act = fdot(g_ref[...], down_ref[cols, :], NT)
-        square = pre * pre
-        tanh_val = jnp.tanh(pre * (GELU_LIN + GELU_CUB * square))
-        cdf = 0.5 + 0.5 * tanh_val
-        slope = cdf + (0.5 * pre) * (1.0 - tanh_val * tanh_val) * (GELU_LIN + 3.0 * GELU_CUB * square)
-        act_ref[:, cols] = (pre * cdf).astype(jnp.bfloat16)
-        dpre_ref[:, cols] = (d_act * slope).astype(jnp.bfloat16)
+        for top in range(0, x_ref.shape[0], SUB):
+            rows = slice(top, top + SUB)
+            pre = fdot(x_ref[rows, :], up_ref[:, cols], NN)
+            d_act = fdot(g_ref[rows, :], down_ref[cols, :], NT)
+            square = pre * pre
+            cdf = 0.5 + 0.5 * jnp.tanh(pre * (GELU_LIN + GELU_CUB * square))
+            act = pre * cdf
+            slope = cdf + (act * (1.0 - cdf)) * (2.0 * GELU_LIN + 6.0 * GELU_CUB * square)
+            act_ref[rows, cols] = act.astype(jnp.bfloat16)
+            dpre_ref[rows, cols] = (d_act * slope).astype(jnp.bfloat16)
 
 
 def act_and_dpre(core, x_all, grad, w_up, w_down, layer):
@@ -114,51 +119,59 @@
     )(core, dpre, *([w_up] * parts), *extra)
 
 
-def token_dot_kernel(left_own, right_own, left_peer, right_peer, out_ref, total):
+def token_dot_kernel(order_ref, left_own, right_own, left_peer, right_peer, out_ref, total):
     k = pl.program_id(2)
+    last = pl.num_programs(2) - 1
+    odd = lax.rem(k, 2)
 
     @pl.when(k == 0)
     def _():
         total[...] = fdot(left_own[...], right_own[...], TN)
 
-    @pl.when(k == 1)
+    @pl.when(jnp.logical_and(k > 0, odd == 0))
     def _():
         total[...] += fdot(left_own[...], right_own[...], TN)
 
-    @pl.when(k == 2)
+    @pl.when(jnp.logical_and(k < last, odd == 1))
     def _():
         total[...] += fdot(left_peer[...], right_peer[...], TN)
 
-    @pl.when(k == 3)
+    @pl.when(k == last)
     def _():
         out_ref[...] = (total[...] + fdot(left_peer[...], right_peer[...], TN)).astype(jnp.bfloat16)
 
 
-def token_dot(left_own, right_own, left_peer, right_peer, tokens, tile, left_row=0):
-    rows, cols = left_own.shape[1], right_own.shape[1]
-    depth = tokens // 2
+def token_dot(order, left_own, right_own, left_peer, right_peer, tokens, tile, left_row=0, cols=None, right_col=0):
+    rows = left_own.shape[1]
+    cols = cols or right_own.shape[1]
     row_tile, col_tile = tile
-
-    def block(width, axis, first, row):
-        def index(i, j, k):
-            step = jnp.minimum(k, 1) if first else jnp.maximum(k - 2, 0)
-            return (row + step, (i, j)[axis])
-        return pl.BlockSpec((depth, width), index)
-
+    steps = tokens // DEPTH
+
+    def left(own):
+        return pl.BlockSpec((DEPTH, row_tile), lambda i, j, k, c: (left_row * steps + (k // 2 if own else jnp.maximum(k - 1, 0) // 2), i))
+
+    def right(own):
+        return pl.BlockSpec((DEPTH, col_tile), lambda i, j, k, c: (k // 2 if own else jnp.maximum(k - 1, 0) // 2, right_col + j))
+
+    spec = pltpu.PrefetchScalarGridSpec(
+        num_scalar_prefetch=1,
+        grid=(rows // row_tile, cols // col_tile, 2 * steps),
+        in_specs=[left(True), right(True), left(False), right(False)],
+        out_specs=pl.BlockSpec((row_tile, col_tile), lambda i, j, k, c: (i, j)),
+        scratch_shapes=[pltpu.VMEM((row_tile, col_tile), jnp.float32)],
+    )
     return pl.pallas_call(
         token_dot_kernel,
         out_shape=jax.ShapeDtypeStruct((rows, cols), jnp.bfloat16),
-        grid=(rows // row_tile, cols // col_tile, 4),
-        in_specs=[block(row_tile, 0, True, left_row), block(col_tile, 1, True, 0), block(row_tile, 0, False, left_row), block(col_tile, 1, False, 0)],
-        out_specs=pl.BlockSpec((row_tile, col_tile), lambda i, j, k: (i, j)),
-        scratch_shapes=[pltpu.VMEM((row_tile, col_tile), jnp.float32)],
+        grid_spec=spec,
         compiler_params=params(),
         cost_estimate=cost(4 * tokens * rows * cols, 4 * tokens * (rows + cols) + 2 * rows * cols),
         name="token_dot",
-    )(left_own, right_own, left_peer, right_peer)
-
-
-def sum_kernel(recv_ref, acc_ref, grad_ref, sq_ref):
+    )(order, left_own, right_own, left_peer, right_peer)
+
+
+def sum_kernel(recv_ref, acc_ref, *refs):
+    grad_ref, sq_ref = refs[-2:]
     total = recv_ref[0].astype(jnp.float32)
     for src in range(1, recv_ref.shape[0]):
         total += recv_ref[src].astype(jnp.float32)
@@ -178,18 +191,32 @@
         sq_ref[...] += square
 
 
-def summed(recv, gacc, layer, grid, recv_block, recv_index, tile, index):
+def summed(recv, gacc, layer, grid, recv_block, recv_index, tile, index, earlier=()):
     rows, cols = gacc.shape[1:]
+    moved = recv.size * 2 + recv.size * 2
     return pl.pallas_call(
         sum_kernel,
         out_shape=[jax.ShapeDtypeStruct((rows, cols), jnp.float32), jax.ShapeDtypeStruct((8, tile[1]), jnp.float32)],
         grid=grid,
-        in_specs=[pl.BlockSpec(recv_block, recv_index), pl.BlockSpec((None,) + tile, lambda a, b: (layer,) + index(a, b))],
+        in_specs=[pl.BlockSpec(recv_block, recv_index), pl.BlockSpec((None,) + tile, lambda a, b: (layer,) + index(a, b))] + [pl.BlockSpec(memory_space=pl.ANY)] * len(earlier),
         out_specs=[pl.BlockSpec(tile, index), pl.BlockSpec((8, tile[1]), lambda a, b: (0, 0))],
-        compiler_params=params(),
-        cost_estimate=cost(8 * rows * cols, 16 * rows * cols),
+        input_output_aliases={2 + i: i for i in range(len(earlier))},
+        compiler_params=params(),
+        cost_estimate=cost(2 * recv.size, moved),
         name="grad_sum",
-    )(recv, gacc)
+    )(recv, gacc, *earlier)
+
+
+def summed_down(recv, gacc, layer, first_col, earlier=()):
+    width = recv.shape[1]
+    tile = (192, 512)
+    skip = first_col // tile[1]
+    return summed(recv.reshape(4, -1, width), gacc, layer, (4, width // tile[1]), (4,) + tile, lambda a, b: (0, a, b), tile, lambda a, b: (a, skip + b), earlier)
+
+
+def summed_up(recv, gacc, layer):
+    tile = (192, FF)
+    return summed(recv.reshape(4, 2, -1, recv.shape[1]), gacc, layer, (4, 2), (4, None) + tile, lambda a, b: (0, b, 0, a), tile, lambda a, b: (0, 2 * a + b))
 
 
 def norm_kernel(n_dev, clip_norm, part_ref, clip_ref, slots, send_sem, recv_sem):
@@ -269,9 +296,11 @@
 def up_kernel(x_ref, w_ref, act_ref):
     for start in range(0, w_ref.shape[1], LANES):
         cols = slice(start, start + LANES)
-        pre = fdot(x_ref[...], w_ref[:, cols], NN)
-        cdf = 0.5 + 0.5 * jnp.tanh(pre * (GELU_LIN + GELU_CUB * (pre * pre)))
-        act_ref[:, cols] = (pre * cdf).astype(jnp.bfloat16)
+        for top in range(0, x_ref.shape[0], SUB):
+            rows = slice(top, top + SUB)
+            pre = fdot(x_ref[rows, :], w_ref[:, cols], NN)
+            cdf = 0.5 + 0.5 * jnp.tanh(pre * (GELU_LIN + GELU_CUB * (pre * pre)))
+            act_ref[rows, cols] = (pre * cdf).astype(jnp.bfloat16)
 
 
 def forward_up(hidden, weight):
@@ -289,7 +318,8 @@
     )(hidden, weight)
 
 
-def down_kernel(act_ref, w_ref, hidden_ref, out_ref, total):
+def down_kernel(act_ref, w_ref, hidden_ref, *refs):
+    out_ref, total = refs[-2:]
     k = pl.program_id(2)
     last = pl.num_programs(2) - 1
 
@@ -306,22 +336,23 @@
         out_ref[...] = (hidden_ref[...].astype(jnp.float32) + (total[...] + fdot(act_ref[...], w_ref[...], NN))).astype(jnp.bfloat16)
 
 
-def forward_down(act, weight, hidden):
+def forward_down(act, weight, hidden, col=0, earlier=()):
     tokens, ff = act.shape
     width = weight.shape[1]
-    col_tile, depth = width // 2, 2 * FF
-    tile = pl.BlockSpec((TOK, col_tile), lambda i, j, k: (i, j))
+    depth = DEPTH * WIDE // width
+    tile = pl.BlockSpec((WIDE, width), lambda i, j, k: (i, col))
     return pl.pallas_call(
         down_kernel,
-        out_shape=jax.ShapeDtypeStruct((tokens, width), jnp.bfloat16),
-        grid=(tokens // TOK, width // col_tile, ff // depth),
-        in_specs=[pl.BlockSpec((TOK, depth), lambda i, j, k: (i, k)), pl.BlockSpec((depth, col_tile), lambda i, j, k: (k, j)), tile],
+        out_shape=jax.ShapeDtypeStruct(hidden.shape, jnp.bfloat16),
+        grid=(tokens // WIDE, 1, ff // depth),
+        in_specs=[pl.BlockSpec((WIDE, depth), lambda i, j, k: (i, k)), pl.BlockSpec((depth, width), lambda i, j, k: (k, 0)), tile] + [pl.BlockSpec(memory_space=pl.ANY)] * len(earlier),
         out_specs=tile,
-        scratch_shapes=[pltpu.VMEM((TOK, col_tile), jnp.float32)],
+        scratch_shapes=[pltpu.VMEM((WIDE, width), jnp.float32)],
+        input_output_aliases={3 + i: i for i in range(len(earlier))},
         compiler_params=params(),
         cost_estimate=cost(2 * tokens * width * ff, 2 * tokens * ff + 4 * tokens * width + 2 * width * ff),
         name="forward_down",
-    )(act, weight, hidden)
+    )(act, weight, hidden, *earlier)
 
 
 def pair_swap(value):
@@ -341,6 +372,7 @@
     x_peer, grad_peer = pair_swap(x_own), pair_swap(grad_own)
     rows_up, rows_down = [None] * layers, [None] * layers
     recv_down = None
+    squares = []
     for layer in range(layers - 1, -1, -1):
         act_own, dpre_own = act_and_dpre(core, x_own, grad_own, w_up, w_down, layer)
         peer_core = after(core, act_own) if recv_down is None else after(core, act_own, recv_down)
@@ -350,13 +382,27 @@
             from_peer = pair_swap(grad_back(core, dpre_peer, w_up, layer))
             grad_own = grad_back(core, dpre_own, w_up, layer, (grad_own, from_peer))
             grad_peer = pair_swap(grad_own)
-        part_down = token_dot(act_own, old_grads[0], act_peer, old_grads[1], tokens, (TOK, FF))
-        recv_down = lax.all_to_all(part_down, "fsdp", 0, 0, tiled=True, axis_index_groups=SAME_CORE)
-        part_up = token_dot(x_own, dpre_own, x_peer, dpre_peer, tokens, (FF, TOK), layer * 2)
+        ranges = [(0, width)] if layer > 0 else [(2 * width // 3, width // 3), (0, 2 * width // 3)]
+        order, partial_sums = core, []
+        for start, cols in ranges:
+            row_tile = WIDE if cols > 512 else 2 * WIDE
+            part = token_dot(order, act_own, old_grads[0], act_peer, old_grads[1], tokens, (row_tile, cols), 0, cols, start // cols)
+            recv_down = lax.all_to_all(part, "fsdp", 0, 0, tiled=True, axis_index_groups=SAME_CORE)
+            partial_sums.append((recv_down, start))
+            order = after(core, part)
+        if len(ranges) > 1:
+            order = after(order, partial_sums[0][0])
+        part_up = token_dot(order, x_own, dpre_own, x_peer, dpre_peer, tokens, (WIDE, WIDE), layer)
         recv_up = lax.all_to_all(part_up, "fsdp", 0, 0, tiled=True)
-        rows_down[layer] = summed(recv_down.reshape(4, -1, width), gacc_down, layer, (4, 1), (4, 192, width), lambda a, b: (0, a, 0), (192, width), lambda a, b: (a, 0))
-        rows_up[layer] = summed(recv_up.reshape(4, 2, -1, ff // 2), gacc_up, layer, (4, 2), (4, None, 192, FF), lambda a, b: (0, b, 0, a), (192, FF), lambda a, b: (0, 2 * a + b))
-    return rows_up, rows_down
+        earlier = ()
+        for recv, start in partial_sums:
+            grad, sq = summed_down(recv, gacc_down, layer, start, earlier)
+            earlier = (grad,)
+            squares.append(sq)
+        rows_down[layer] = grad
+        rows_up[layer], sq = summed_up(recv_up, gacc_up, layer)
+        squares.append(sq)
+    return rows_up, rows_down, squares
 
 
 def solution(mesh):
@@ -366,20 +412,26 @@
     def local_step(x_saved, grad_out, x_next, w_up, w_down, gacc_up, gacc_down, master_up, master_down, mom1_up, mom1_down, mom2_up, mom2_down):
         layers, width, ff = w_up.shape
         clip_norm = 0.1 * math.sqrt(2 * layers * width * ff)
-        rows_up, rows_down = gradient_rows(x_saved, grad_out, w_up, w_down, gacc_up, gacc_down)
-        part = sum(jnp.sum(sq.reshape(8, -1, 128), axis=1) for _, sq in rows_up + rows_down)
+        rows_up, rows_down, squares = gradient_rows(x_saved, grad_out, w_up, w_down, gacc_up, gacc_down)
+        part = sum(jnp.sum(sq.reshape(8, -1, 128), axis=1) for sq in squares)
         clip = clip_factor(part, n_dev, clip_norm)
         new_up, new_down = (), ()
         up_shards, down_shards = [], []
         for layer in range(layers):
-            *new_up, shard = adamw(clip, rows_up[layer][0], master_up, mom1_up, mom2_up, layer, (192, FF), new_up)
+            *new_up, shard = adamw(clip, rows_up[layer], master_up, mom1_up, mom2_up, layer, (96, FF), new_up)
             up_shards.append(shard)
-            *new_down, shard = adamw(clip, rows_down[layer][0], master_down, mom1_down, mom2_down, layer, (96, width), new_down)
+            *new_down, shard = adamw(clip, rows_down[layer], master_down, mom1_down, mom2_down, layer, (48, width), new_down)
             down_shards.append(shard)
         hidden = x_next.reshape(-1, width)
         for layer in range(layers):
             act = forward_up(hidden, lax.all_gather(up_shards[layer], "fsdp", axis=0, tiled=True))
-            hidden = forward_down(act, lax.all_gather(down_shards[layer], "fsdp", axis=0, tiled=True), hidden)
+            parts = 1 if layer < layers - 1 else 2
+            cols = width // parts
+            new_hidden = ()
+            for part in range(parts):
+                weight = lax.all_gather(down_shards[layer][:, part * cols:(part + 1) * cols], "fsdp", axis=0, tiled=True)
+                new_hidden = (forward_down(act, weight, hidden, part, new_hidden),)
+            hidden = new_hidden[0]
         return (hidden.reshape(x_next.shape), new_up[0], new_down[0], new_up[1], new_down[1], new_up[2], new_down[2])
 
     return jax.shard_map(local_step, mesh=mesh, in_specs=(rows_spec, P("fsdp"), P("fsdp"), P(), P(), rows_spec, rows_spec, rows_spec, rows_spec, rows_spec, rows_spec, rows_spec, rows_spec), out_specs=(P("fsdp"), rows_spec, rows_spec, rows_spec, rows_spec, rows_spec, rows_spec), check_vma=False)

time: 1370 us -> 1270 us (0.927)
  waiting for transfers between devices: 211 us -> 155 us
  Pallas kernels: 1110 us -> 1060 us
    pallas_call x4, Pallas kernels: 312 us -> 277 us  [act_and_dpre(): pl.pallas_call(act_dpre_kernel, out_shape=[jax.ShapeDtypeStruct((tokens,...]
    pallas_call x4 -> x5, Pallas kernels: 328 us -> 299 us  [token_dot(): pl.pallas_call(token_dot_kernel, out_shape=jax.ShapeDtypeStruct((rows, co...]
    all_to_all x2 -> x3, waiting for transfers between devices: 24 us -> 0.01 us  [gradient_rows(): lax.all_to_all(part, 'fsdp', 0, 0, tiled=True, axis_index_groups=SAME_CORE)]
    all_gather x2 -> x3, waiting for transfers between devices: 39.1 us -> 25.4 us  [local_step(): lax.all_gather(down_shards[layer][:, part * cols:(part + 1) * cols], 'fsd...]
    pallas_call x4 -> x5, Pallas kernels: 34.7 us -> 42.4 us  [summed(): pl.pallas_call(sum_kernel, out_shape=[jax.ShapeDtypeStruct((rows, cols),...]
    pallas_call x2 -> x3, Pallas kernels: 142 us -> 142 us  [forward_down(): pl.pallas_call(down_kernel, out_shape=jax.ShapeDtypeStruct(hidden.shape,...]
  transfers between devices with their start and end apart: 12 -> 14, of which waited for: 6 -> 5; matrix products, arithmetic and copies ran while one was open for 0% -> 0% of each run, Pallas kernels for 66% -> 70%
where the time goes in v2:
time: 1270 us; the launch traced here: 1260 us
  Pallas kernels  1060 us (83%)
  waiting for transfers between devices  155 us (12%)
  starting transfers between devices  25.6 us (2%)
  between operations  14.3 us (1%)
    pallas_call x5, Pallas kernels, token_dot(): pl.pallas_call(token_dot_kernel, out_shape=jax.ShapeDtypeStruct((rows, co...  299 us
    pallas_call x4, Pallas kernels, act_and_dpre(): pl.pallas_call(act_dpre_kernel, out_shape=[jax.ShapeDtypeStruct((tokens,...  277 us
    pallas_call x2, Pallas kernels, forward_up(): pl.pallas_call(up_kernel, out_shape=jax.ShapeDtypeStruct((tokens, ff), jn...  143 us
    pallas_call x3, Pallas kernels, forward_down(): pl.pallas_call(down_kernel, out_shape=jax.ShapeDtypeStruct(hidden.shape,...  142 us
    pallas_call x2, Pallas kernels, grad_back(): pl.pallas_call(functools.partial(back_kernel, parts, bool(extra)), out_sh...  76.1 us
    pallas_call x4, Pallas kernels, adamw(): pl.pallas_call(functools.partial(adamw_kernel, len(earlier)), out_shape=[...  74.7 us
    all_to_all x2, waiting for transfers between devices, gradient_rows(): recv_up = lax.all_to_all(part_up, 'fsdp', 0, 0, tiled=True)  70.8 us
    all_gather x2, waiting for transfers between devices, local_step(): lax.all_gather(up_shards[layer], 'fsdp', axis=0, tiled=True)  58.6 us
  transfers between devices with their start and end apart: 14, of which 5 were waited for; matrix products, arithmetic and copies ran while one was open for 0% of the time, Pallas kernels for 70%

profile of v2, /device:TPU:0, one launch (start us, length us, event | category | flops | bytes accessed | tf_op | source)
XLA Modules:
  0.0 1260.8 jit_solution(4306878446461629205)
XLA Ops:
  8.1 69.2 %act_dpre.4 = (bf16[3072,3072]{1,0:T(8,128)(2,1)}, bf16[3072,3072]{1,0:T(8,128)(2,1)}) custom-call(s32[1]{0:T(128)} %bitcast.1.core_ref.order_ref, bf16[6144,1536]{1,0:T(8,128)(2,1)} %bitcast.32, bf16[3072,1536]{1,0:T(8,128)(2,1)} %bitcast.23, bf16[2,1536,6144]{2,1,0:T(8,128)(2,1)} %up_ref.7, bf16[2,6144,1536]{2,1,0:T(8,128)(2,1)} %down_ref.7), custom_call_target="tpu_custom_call" | custom-call | flops 57982058496 | bytes 113246208 | tf_op jit(solution)/shard_map/act_dpre/pallas_call | solution.py:76
  77.3 69.5 %act_dpre.5 = (bf16[3072,3072]{1,0:T(8,128)(2,1)}, bf16[3072,3072]{1,0:T(8,128)(2,1)}) custom-call(s32[1]{0:T(128)} %bitcast.1.core_ref.order_ref, bf16[6144,1536]{1,0:T(8,128)(2,1)} %collective-permute-done.x_ref.left_peer, bf16[3072,1536]{1,0:T(8,128)(2,1)} %collective-permute-done.1.g_ref.right_peer, bf16[2,1536,6144]{2,1,0:T(8,128)(2,1)} %up_ref.7, ...), custom_call_target="tpu_custom_call" | custom-call | flops 57982058496 | bytes 113246208 | tf_op jit(solution)/shard_map/act_dpre/pallas_call | solution.py:76
  146.7 37.0 %grad_back.2 = f32[3072,1536]{1,0:T(8,128)} custom-call(s32[1]{0:T(128)} %bitcast.1.core_ref.order_ref, bf16[3072,3072]{1,0:T(8,128)(2,1)} %get-tuple-element.52.right_peer.dpre_ref, bf16[2,1536,6144]{2,1,0:T(8,128)(2,1)} %up_ref.7, bf16[2,1536,6144]{2,1,0:T(8,128)(2,1)} %up_ref.7, bf16[2,1536,6144]{2,1,0:T(8,128)(2,1)} %up_ref.7, bf16[2,1536,6144]{2,1,0:T(8,128)(2,1)} %up_ref.7), custom_call_target="tpu_custom_call" | custom-call | flops 28991029248 | bytes 66060288 | tf_op jit(solution)/shard_map/grad_back/pallas_call | solution.py:112
  184.2 80.6 %token_dot.5 = bf16[3072,1536]{1,0:T(8,128)(2,1)} custom-call(s32[1]{0:T(128)} %bitcast.1.core_ref.order_ref, bf16[3072,3072]{1,0:T(8,128)(2,1)} %get-tuple-element.46.left_own, bf16[3072,1536]{1,0:T(8,128)(2,1)} %bitcast.24, bf16[3072,3072]{1,0:T(8,128)(2,1)} %get-tuple-element.48.left_peer, bf16[3072,1536]{1,0:T(8,128)(2,1)} %collective-permute-done.1.g_ref.right_peer), custom_call_target="tpu_custom_call" | custom-call | flops 57982058496 | bytes 66060288 | tf_op jit(solution)/shard_map/token_dot/pallas_call | solution.py:163
  264.8 5.8 all-to-all-start
  270.6 39.2 %grad_back.3.g_ref.right_own = bf16[3072,1536]{1,0:T(8,128)(2,1)} custom-call(s32[1]{0:T(128)} %bitcast.1.core_ref.order_ref, bf16[3072,3072]{1,0:T(8,128)(2,1)} %get-tuple-element.51.right_own.dpre_ref, bf16[2,1536,6144]{2,1,0:T(8,128)(2,1)} %up_ref.7, bf16[2,1536,6144]{2,1,0:T(8,128)(2,1)} %up_ref.7, bf16[2,1536,6144]{2,1,0:T(8,128)(2,1)} %up_ref.7, ...), custom_call_target="tpu_custom_call" | custom-call | flops 28991029248 | bytes 66060288 | tf_op jit(solution)/shard_map/grad_back/pallas_call | solution.py:112
  309.9 70.0 %token_dot.6 = bf16[1536,3072]{1,0:T(8,128)(2,1)} custom-call(s32[1]{0:T(128)} %bitcast.1.core_ref.order_ref, bf16[6144,1536]{1,0:T(8,128)(2,1)} %bitcast.33, bf16[3072,3072]{1,0:T(8,128)(2,1)} %get-tuple-element.51.right_own.dpre_ref, bf16[6144,1536]{1,0:T(8,128)(2,1)} %collective-permute-done.x_ref.left_peer, ...), custom_call_target="tpu_custom_call" | custom-call | flops 57982058496 | bytes 66060288 | tf_op jit(solution)/shard_map/token_dot/pallas_call | solution.py:163
  383.8 69.1 %act_dpre.6 = (bf16[3072,3072]{1,0:T(8,128)(2,1)}, bf16[3072,3072]{1,0:T(8,128)(2,1)}) custom-call(s32[1]{0:T(128)} %bitcast.1.core_ref.order_ref, bf16[6144,1536]{1,0:T(8,128)(2,1)} %bitcast.34, bf16[3072,1536]{1,0:T(8,128)(2,1)} %grad_back.3.g_ref.right_own, bf16[2,1536,6144]{2,1,0:T(8,128)(2,1)} %up_ref.7, bf16[2,6144,1536]{2,1,0:T(8,128)(2,1)} %down_ref.7), custom_call_target="tpu_custom_call" | custom-call | flops 57982058496 | bytes 113246208 | tf_op jit(solution)/shard_map/act_dpre/pallas_call | solution.py:76
  452.8 69.3 %act_dpre.7 = (bf16[3072,3072]{1,0:T(8,128)(2,1)}, bf16[3072,3072]{1,0:T(8,128)(2,1)}) custom-call(s32[1]{0:T(128)} %bitcast.1.core_ref.order_ref, bf16[6144,1536]{1,0:T(8,128)(2,1)} %collective-permute-done.x_ref.left_peer, bf16[3072,1536]{1,0:T(8,128)(2,1)} %collective-permute-done.3.g_ref.right_peer, bf16[2,1536,6144]{2,1,0:T(8,128)(2,1)} %up_ref.7, ...), custom_call_target="tpu_custom_call" | custom-call | flops 57982058496 | bytes 113246208 | tf_op jit(solution)/shard_map/act_dpre/pallas_call | solution.py:76
  522.2 28.0 %token_dot.7 = bf16[3072,512]{1,0:T(8,128)(2,1)} custom-call(s32[1]{0:T(128)} %bitcast.1.core_ref.order_ref, bf16[3072,3072]{1,0:T(8,128)(2,1)} %get-tuple-element.54.left_own, bf16[3072,1536]{1,0:T(8,128)(2,1)} %grad_back.3.g_ref.right_own, bf16[3072,3072]{1,0:T(8,128)(2,1)} %get-tuple-element.56.left_peer, ...), custom_call_target="tpu_custom_call" | custom-call | flops 19327352832 | bytes 47185920 | tf_op jit(solution)/shard_map/token_dot/pallas_call | solution.py:163
  550.2 5.2 all-to-all-start.2
  555.4 49.7 %token_dot.8 = bf16[3072,1024]{1,0:T(8,128)(2,1)} custom-call(s32[1]{0:T(128)} %bitcast.1.core_ref.order_ref, bf16[3072,3072]{1,0:T(8,128)(2,1)} %get-tuple-element.54.left_own, bf16[3072,1536]{1,0:T(8,128)(2,1)} %grad_back.3.g_ref.right_own, bf16[3072,3072]{1,0:T(8,128)(2,1)} %get-tuple-element.56.left_peer, ...), custom_call_target="tpu_custom_call" | custom-call | flops 38654705664 | bytes 56623104 | tf_op jit(solution)/shard_map/token_dot/pallas_call | solution.py:163
  605.0 5.3 all-to-all-start.3
  610.3 70.3 %token_dot.9 = bf16[1536,3072]{1,0:T(8,128)(2,1)} custom-call(s32[1]{0:T(128)} %bitcast.1.core_ref.order_ref, bf16[6144,1536]{1,0:T(8,128)(2,1)} %bitcast.35, bf16[3072,3072]{1,0:T(8,128)(2,1)} %get-tuple-element.62.right_own, bf16[6144,1536]{1,0:T(8,128)(2,1)} %collective-permute-done.x_ref.left_peer, bf16[3072,3072]{1,0:T(8,128)(2,1)} %get-tuple-element.63.right_peer), custom_call_target="tpu_custom_call" | custom-call | flops 57982058496 | bytes 66060288 | tf_op jit(solution)/shard_map/token_dot/pallas_call | solution.py:163
  684.5 11.1 grad_sum.5
  696.4 9.6 grad_sum.6
  710.4 7.8 grad_sum.8
  718.9 70.8 %all-to-all-done.4 = bf16[8,192,3072]{2,1,0:T(8,128)(2,1)} async-done(((bf16[8,192,3072]{2,1,0:T(8,128)(2,1)}), bf16[8,192,3072]{2,1,0:T(8,128)(2,1)}, u32[]{:S(2)}, u32[]{:S(2)}) %all-to-all-start.4) | async-done | bytes 9437216 | tf_op jit(solution)/shard_map/all_to_all | solution.py:396
  789.7 9.5 grad_sum.9
  800.6 6.1 clip_norm.1.clip_ref
  806.7 18.7 %adamw.4 = (f32[2,192,6144]{2,1,0:T(8,128)}, f32[2,192,6144]{2,1,0:T(8,128)}, f32[2,192,6144]{2,1,0:T(8,128)}, bf16[192,6144]{1,0:T(8,128)(2,1)}) custom-call(f32[8,128]{1,0:T(8,128)} %clip_norm.1.clip_ref, f32[192,6144]{1,0:T(8,128)} %get-tuple-element.65.grad_ref, f32[2,192,6144]{2,1,0:T(8,128)} %master_ref.6, f32[2,192,6144]{2,1,0:T(8,128)} %one_ref.6, ...), custom_call_target="tpu_custom_call" | custom-call | flops 23592960 | bytes 35389440 | tf_op jit(solution)/shard_map/adamw/pallas_call | solution.py:283
  825.5 18.6 %adamw.5 = (f32[2,768,1536]{2,1,0:T(8,128)}, f32[2,768,1536]{2,1,0:T(8,128)}, f32[2,768,1536]{2,1,0:T(8,128)}, bf16[768,1536]{1,0:T(8,128)(2,1)}) custom-call(f32[8,128]{1,0:T(8,128)} %clip_norm.1.clip_ref, f32[768,1536]{1,0:T(8,128)} %get-tuple-element.67.grad_ref, f32[2,768,1536]{2,1,0:T(8,128)} %master_ref.7, f32[2,768,1536]{2,1,0:T(8,128)} %one_ref.7, ...), custom_call_target="tpu_custom_call" | custom-call | flops 23592960 | bytes 35389440 | tf_op jit(solution)/shard_map/adamw/pallas_call | solution.py:283
  844.2 18.7 %adamw.6 = (f32[2,192,6144]{2,1,0:T(8,128)}, f32[2,192,6144]{2,1,0:T(8,128)}, f32[2,192,6144]{2,1,0:T(8,128)}, bf16[192,6144]{1,0:T(8,128)(2,1)}) custom-call(f32[8,128]{1,0:T(8,128)} %clip_norm.1.clip_ref, f32[192,6144]{1,0:T(8,128)} %get-tuple-element.69.grad_ref, ...), custom_call_target="tpu_custom_call", output_to_operand_aliasing={{0}: (5, {}), {1}: (6, {}), {2}: (7, {})} | custom-call | flops 23592960 | bytes 35389440 | tf_op jit(solution)/shard_map/adamw/pallas_call | solution.py:283
  863.0 18.7 %adamw.7 = (f32[2,768,1536]{2,1,0:T(8,128)}, f32[2,768,1536]{2,1,0:T(8,128)}, f32[2,768,1536]{2,1,0:T(8,128)}, bf16[768,1536]{1,0:T(8,128)(2,1)}) custom-call(f32[8,128]{1,0:T(8,128)} %clip_norm.1.clip_ref, f32[768,1536]{1,0:T(8,128)} %get-tuple-element.74.grad_ref, ...), custom_call_target="tpu_custom_call", output_to_operand_aliasing={{0}: (5, {}), {1}: (6, {}), {2}: (7, {})} | custom-call | flops 23592960 | bytes 35389440 | tf_op jit(solution)/shard_map/adamw/pallas_call | solution.py:283
  885.4 32.3 %all-gather.6.cloned.1.call-done.w_ref = bf16[1536,6144]{1,0:T(8,128)(2,1)} async-done(((bf16[192,6144]{1,0:T(8,128)(2,1)}), bf16[1536,6144]{1,0:T(8,128)(2,1)}) %all-gather.6.cloned.1.call-update) | async-done | bytes 18874384 | tf_op jit(solution)/shard_map/all_gather | solution.py:427
  917.7 71.3 %forward_up.2.act_ref = bf16[3072,6144]{1,0:T(8,128)(2,1)} custom-call(bf16[3072,1536]{1,0:T(8,128)(2,1)} %bitcast.36, bf16[1536,6144]{1,0:T(8,128)(2,1)} %all-gather.6.cloned.1.call-done.w_ref), custom_call_target="tpu_custom_call" | custom-call | flops 57982058496 | bytes 66060288 | tf_op jit(solution)/shard_map/forward_up/pallas_call | solution.py:309
  989.0 24.1 %all-gather.8.cloned.1.call-done.w_ref = bf16[6144,1536]{1,0:T(8,128)(2,1)} async-done(((bf16[768,1536]{1,0:T(8,128)(2,1)}), bf16[6144,1536]{1,0:T(8,128)(2,1)}) %all-gather.8.cloned.1.call-update) | async-done | bytes 18874384 | tf_op jit(solution)/shard_map/all_gather | solution.py:432
  1013.1 68.6 %forward_down.3.x_ref.hidden_ref = bf16[3072,1536]{1,0:T(8,128)(2,1)} custom-call(bf16[3072,6144]{1,0:T(8,128)(2,1)} %forward_up.2.act_ref, bf16[6144,1536]{1,0:T(8,128)(2,1)} %all-gather.8.cloned.1.call-done.w_ref, bf16[3072,1536]{1,0:T(8,128)(2,1)} %bitcast.37), custom_call_target="tpu_custom_call" | custom-call | flops 57982058496 | bytes 75497472 | tf_op jit(solution)/shard_map/forward_down/pallas_call | solution.py:344
  1081.6 26.3 %all-gather.10.cloned.1.call-done.w_ref = bf16[1536,6144]{1,0:T(8,128)(2,1)} async-done(((bf16[192,6144]{1,0:T(8,128)(2,1)}), bf16[1536,6144]{1,0:T(8,128)(2,1)}) %all-gather.10.cloned.1.call-update) | async-done | bytes 18874384 | tf_op jit(solution)/shard_map/all_gather | solution.py:427
  1107.9 71.5 %forward_up.3.act_ref = bf16[3072,6144]{1,0:T(8,128)(2,1)} custom-call(bf16[3072,1536]{1,0:T(8,128)(2,1)} %forward_down.3.x_ref.hidden_ref, bf16[1536,6144]{1,0:T(8,128)(2,1)} %all-gather.10.cloned.1.call-done.w_ref), custom_call_target="tpu_custom_call" | custom-call | flops 57982058496 | bytes 66060288 | tf_op jit(solution)/shard_map/forward_up/pallas_call | solution.py:309
  1179.4 36.4 %forward_down.4.refs_0_ = bf16[3072,1536]{1,0:T(8,128)(2,1)} custom-call(bf16[3072,6144]{1,0:T(8,128)(2,1)} %forward_up.3.act_ref, bf16[6144,768]{1,0:T(8,128)(2,1)} %all-gather.14.cloned.1.call-done.w_ref, bf16[3072,1536]{1,0:T(8,128)(2,1)} %forward_down.3.x_ref.hidden_ref), custom_call_target="tpu_custom_call" | custom-call | flops 28991029248 | bytes 56623104 | tf_op jit(solution)/shard_map/forward_down/pallas_call | solution.py:344
  1217.2 36.7 %forward_down.5 = bf16[3072,1536]{1,0:T(8,128)(2,1)} custom-call(bf16[3072,6144]{1,0:T(8,128)(2,1)} %forward_up.3.act_ref, bf16[6144,768]{1,0:T(8,128)(2,1)} %all-gather.12.cloned.1.call-done.w_ref, bf16[3072,1536]{1,0:T(8,128)(2,1)} %forward_down.3.x_ref.hidden_ref, bf16[3072,1536]{1,0:T(8,128)(2,1)} %forward_down.4.refs_0_), custom_call_target="tpu_custom_call", output_to_operand_aliasing={{}: (3, {})} | custom-call | flops 28991029248 | bytes 56623104 | tf_op jit(solution)/shard_map/forward_down/pallas_call | solution.py:344
  (38 shorter events, 21.7 us)
Async XLA Ops:
  7.2 70.1 %collective-permute-start = (bf16[6144,1536]{1,0:T(8,128)(2,1)}, bf16[6144,1536]{1,0:T(8,128)(2,1)}, u32[]{:S(2)}, u32[]{:S(2)}) collective-permute-start(bf16[6144,1536]{1,0:T(8,128)(2,1)} %bitcast.31), channel_id=1, source_target_pairs={{0,1},{1,0},{2,3},{3,2},{4,5},{5,4},{6,7},{7,6}} | collective-permute-start | bytes 56623112 | tf_op jit(solution)/shard_map/ppermute | solution.py:359
  8.0 69.2 %collective-permute-start.1 = (bf16[3072,1536]{1,0:T(8,128)(2,1)}, bf16[3072,1536]{1,0:T(8,128)(2,1)}, u32[]{:S(2)}, u32[]{:S(2)}) collective-permute-start(bf16[3072,1536]{1,0:T(8,128)(2,1)} %bitcast.22), channel_id=1, source_target_pairs={{0,1},{1,0},{2,3},{3,2},{4,5},{5,4},{6,7},{7,6}} | collective-permute-start | bytes 28311560 | tf_op jit(solution)/shard_map/ppermute | solution.py:359
  183.7 86.9 %collective-permute-start.2 = (f32[3072,1536]{1,0:T(8,128)}, f32[3072,1536]{1,0:T(8,128)}, u32[]{:S(2)}, u32[]{:S(2)}) collective-permute-start(f32[3072,1536]{1,0:T(8,128)} %grad_back.2), channel_id=1, source_target_pairs={{0,1},{1,0},{2,3},{3,2},{4,5},{5,4},{6,7},{7,6}} | collective-permute-start | bytes 56623112 | tf_op jit(solution)/shard_map/ppermute | solution.py:359
  264.8 115.0 %all-to-all-start = ((bf16[4,768,1536]{2,1,0:T(8,128)(2,1)}), bf16[4,768,1536]{2,1,0:T(8,128)(2,1)}, u32[]{:S(2)}, u32[]{:S(2)}) async-start(bf16[4,768,1536]{2,1,0:T(8,128)(2,1)} %bitcast.27), calls=%async_computation | async-start | bytes 18874368 | tf_op jit(solution)/shard_map/all_to_all | solution.py:390
  309.8 143.0 %collective-permute-start.3 = (bf16[3072,1536]{1,0:T(8,128)(2,1)}, bf16[3072,1536]{1,0:T(8,128)(2,1)}, u32[]{:S(2)}, u32[]{:S(2)}) collective-permute-start(bf16[3072,1536]{1,0:T(8,128)(2,1)} %grad_back.3.g_ref.right_own), channel_id=1, source_target_pairs={{0,1},{1,0},{2,3},{3,2},{4,5},{5,4},{6,7},{7,6}} | collective-permute-start | bytes 28311560 | tf_op jit(solution)/shard_map/ppermute | solution.py:359
  379.9 170.3 %all-to-all-start.1 = ((bf16[8,192,3072]{2,1,0:T(8,128)(2,1)}), bf16[8,192,3072]{2,1,0:T(8,128)(2,1)}, u32[]{:S(2)}, u32[]{:S(2)}) async-start(bf16[8,192,3072]{2,1,0:T(8,128)(2,1)} %bitcast.28), calls=%async_computation.1 | async-start | bytes 18874368 | tf_op jit(solution)/shard_map/all_to_all | solution.py:396
  550.2 54.8 %all-to-all-start.2 = ((bf16[4,768,512]{2,1,0:T(8,128)(2,1)}), bf16[4,768,512]{2,1,0:T(8,128)(2,1)S(1)}, u32[]{:S(2)}, u32[]{:S(2)}) async-start(bf16[4,768,512]{2,1,0:T(8,128)(2,1)} %bitcast.30), calls=%async_computation.2 | async-start | bytes 6291456 | tf_op jit(solution)/shard_map/all_to_all | solution.py:390
  605.0 75.6 %copy-start = (bf16[4,768,512]{2,1,0:T(8,128)(2,1)}, bf16[4,768,512]{2,1,0:T(8,128)(2,1)S(1)}, u32[]{:S(2)}) copy-start(bf16[4,768,512]{2,1,0:T(8,128)(2,1)S(1)} %all-to-all-done.2.recv_ref) | copy-start | bytes 9437188
  605.0 75.6 %all-to-all-start.3 = ((bf16[4,768,1024]{2,1,0:T(8,128)(2,1)}), bf16[4,768,1024]{2,1,0:T(8,128)(2,1)}, u32[]{:S(2)}, u32[]{:S(2)}) async-start(bf16[4,768,1024]{2,1,0:T(8,128)(2,1)} %bitcast.29), calls=%async_computation.3 | async-start | bytes 12582912 | tf_op jit(solution)/shard_map/all_to_all | solution.py:390
  680.7 109.0 %all-to-all-start.4 = ((bf16[8,192,3072]{2,1,0:T(8,128)(2,1)}), bf16[8,192,3072]{2,1,0:T(8,128)(2,1)}, u32[]{:S(2)}, u32[]{:S(2)}) async-start(bf16[8,192,3072]{2,1,0:T(8,128)(2,1)} %bitcast.26), calls=%async_computation.4 | async-start | bytes 18874368 | tf_op jit(solution)/shard_map/all_to_all | solution.py:396
  684.5 233.2 %all-gather.6.cloned.1.call-start = ((), (), s32[]{:S(2)}) async-start(), calls=%async_computation.5 | async-start | bytes 21233664 | tf_op jit(solution)/shard_map/all_gather | solution.py:427
  710.4 7.8 copy-start.2
  789.7 9.5 copy-start.1
  825.4 187.7 %all-gather.8.cloned.1.call-start = ((), (), s32[]{:S(2)}) async-start(), calls=%async_computation.6 | async-start | bytes 21233664 | tf_op jit(solution)/shard_map/all_gather | solution.py:432
  844.1 263.8 %all-gather.10.cloned.1.call-start = ((), (), s32[]{:S(2)}) async-start(), calls=%async_computation.7 | async-start | bytes 21233664 | tf_op jit(solution)/shard_map/all_gather | solution.py:427
  862.9 316.5 %all-gather.14.cloned.1.call-start = ((), (), s32[]{:S(2)}) async-start(), calls=%async_computation.9 | async-start | bytes 10616832 | tf_op jit(solution)/shard_map/all_gather | solution.py:432
  884.8 332.4 %all-gather.12.cloned.1.call-start = ((), (), s32[]{:S(2)}) async-start(), calls=%async_computation.8 | async-start | bytes 10616832 | tf_op jit(solution)/shard_map/all_gather | solution.py:432
Sparse Core Ops, SparseCore 0:
  825.5 92.1 all-gather.5
  920.1 92.9 all-gather.7
  1014.9 92.9 all-gather.9
  1109.6 52.9 all-gather.13
  1164.2 52.9 all-gather.11

commit v3 on v2

--- a/solution.py
+++ b/solution.py
@@ -170,17 +170,19 @@
     )(order, left_own, right_own, left_peer, right_peer)
 
 
-def sum_kernel(recv_ref, acc_ref, *refs):
+def sum_kernel(halves, recv_ref, acc_ref, *refs):
     grad_ref, sq_ref = refs[-2:]
-    total = recv_ref[0].astype(jnp.float32)
-    for src in range(1, recv_ref.shape[0]):
-        total += recv_ref[src].astype(jnp.float32)
-    grad = (acc_ref[...] + total) * (1.0 / MICRO_STEPS)
-    grad_ref[...] = grad
-    square = jnp.sum((grad * grad).reshape(-1, 8, grad.shape[1]), axis=0)
-    first = pl.program_id(0) == 0
-    for axis in range(1, 2):
-        first = jnp.logical_and(first, pl.program_id(axis) == 0)
+    cols = acc_ref.shape[1] // halves
+    square = jnp.zeros((8, cols), jnp.float32)
+    for half in range(halves):
+        total = (recv_ref[0, half] if halves > 1 else recv_ref[0]).astype(jnp.float32)
+        for src in range(1, recv_ref.shape[0]):
+            total += (recv_ref[src, half] if halves > 1 else recv_ref[src]).astype(jnp.float32)
+        part = slice(half * cols, (half + 1) * cols)
+        grad = (acc_ref[:, part] + total) * (1.0 / MICRO_STEPS)
+        grad_ref[:, part] = grad
+        square += jnp.sum((grad * grad).reshape(-1, 8, cols), axis=0)
+    first = jnp.logical_and(pl.program_id(0) == 0, pl.program_id(1) == 0)
 
     @pl.when(first)
     def _():
@@ -191,15 +193,15 @@
         sq_ref[...] += square
 
 
-def summed(recv, gacc, layer, grid, recv_block, recv_index, tile, index, earlier=()):
+def summed(recv, gacc, layer, grid, recv_block, recv_index, tile, index, earlier=(), halves=1):
     rows, cols = gacc.shape[1:]
     moved = recv.size * 2 + recv.size * 2
     return pl.pallas_call(
-        sum_kernel,
-        out_shape=[jax.ShapeDtypeStruct((rows, cols), jnp.float32), jax.ShapeDtypeStruct((8, tile[1]), jnp.float32)],
+        functools.partial(sum_kernel, halves),
+        out_shape=[jax.ShapeDtypeStruct((rows, cols), jnp.float32), jax.ShapeDtypeStruct((8, tile[1] // halves), jnp.float32)],
         grid=grid,
         in_specs=[pl.BlockSpec(recv_block, recv_index), pl.BlockSpec((None,) + tile, lambda a, b: (layer,) + index(a, b))] + [pl.BlockSpec(memory_space=pl.ANY)] * len(earlier),
-        out_specs=[pl.BlockSpec(tile, index), pl.BlockSpec((8, tile[1]), lambda a, b: (0, 0))],
+        out_specs=[pl.BlockSpec(tile, index), pl.BlockSpec((8, tile[1] // halves), lambda a, b: (0, 0))],
         input_output_aliases={2 + i: i for i in range(len(earlier))},
         compiler_params=params(),
         cost_estimate=cost(2 * recv.size, moved),
@@ -215,8 +217,8 @@
 
 
 def summed_up(recv, gacc, layer):
-    tile = (192, FF)
-    return summed(recv.reshape(4, 2, -1, recv.shape[1]), gacc, layer, (4, 2), (4, None) + tile, lambda a, b: (0, b, 0, a), tile, lambda a, b: (0, 2 * a + b))
+    tile = (192, 2 * FF)
+    return summed(recv.reshape(4, 2, -1, recv.shape[1]), gacc, layer, (4, 1), (4, 2, 192, FF), lambda a, b: (0, 0, 0, a), tile, lambda a, b: (0, a), (), 2)
 
 
 def norm_kernel(n_dev, clip_norm, part_ref, clip_ref, slots, send_sem, recv_sem):
@@ -259,8 +261,7 @@
     )(part)
 
 
-def adamw_kernel(aliased, clip_ref, grad_ref, master_ref, one_ref, two_ref, *refs):
-    new_master_ref, new_one_ref, new_two_ref, weight_ref = refs[aliased:]
+def adamw_values(clip_ref, grad_ref, master_ref, one_ref, two_ref):
     grad = grad_ref[...] * clip_ref[0:1, 0:1]
     master = master_ref[...]
     one = BETA_ONE * one_ref[...] + (1.0 - BETA_ONE) * grad
@@ -268,27 +269,33 @@
     first_hat = one / (1.0 - BETA_ONE ** ADAM_STEP)
     second_hat = two / (1.0 - BETA_TWO ** ADAM_STEP)
     master = master - LEARN_RATE * (first_hat / (jnp.sqrt(second_hat) + ADAM_EPS) + WEIGHT_DECAY * master)
-    new_one_ref[...] = one
-    new_two_ref[...] = two
-    new_master_ref[...] = master
-    weight_ref[...] = master.astype(jnp.bfloat16)
-
-
-def adamw(clip, grad, master, mom_one, mom_two, layer, tile, earlier=()):
+    return master, one, two
+
+
+def adamw_kernel(aliased, weight, state, *refs):
+    outs = list(refs[5 + aliased:])
+    master, one, two = adamw_values(*refs[:5])
+    if state:
+        for value in (master, one, two):
+            outs.pop(0)[...] = value
+    if weight:
+        outs.pop(0)[...] = master.astype(jnp.bfloat16)
+
+
+def adamw(clip, grad, master, mom_one, mom_two, layer, tile, earlier=(), weight=True, state=True):
     rows, cols = grad.shape
-    index = lambda a, b: (a, b)
     whole = pl.BlockSpec((None,) + tile, lambda a, b: (layer, a, b))
-    part = pl.BlockSpec(tile, index)
+    part = pl.BlockSpec(tile, lambda a, b: (a, b))
     full = jax.ShapeDtypeStruct(master.shape, jnp.float32)
     return pl.pallas_call(
-        functools.partial(adamw_kernel, len(earlier)),
-        out_shape=[full] * 3 + [jax.ShapeDtypeStruct((rows, cols), jnp.bfloat16)],
+        functools.partial(adamw_kernel, len(earlier), weight, state),
+        out_shape=[full] * (3 * state) + [jax.ShapeDtypeStruct((rows, cols), jnp.bfloat16)] * weight,
         grid=(rows // tile[0], cols // tile[1]),
         in_specs=[pl.BlockSpec((8, 128), lambda a, b: (0, 0)), part, whole, whole, whole] + [pl.BlockSpec(memory_space=pl.ANY)] * len(earlier),
-        out_specs=[whole] * 3 + [part],
+        out_specs=[whole] * (3 * state) + [part] * weight,
         input_output_aliases={5 + i: i for i in range(len(earlier))},
         compiler_params=params(),
-        cost_estimate=cost(20 * rows * cols, 30 * rows * cols, 2 * rows * cols),
+        cost_estimate=cost(20 * rows * cols, 16 * rows * cols + 12 * rows * cols * state, 2 * rows * cols),
         name="adamw",
     )(clip, grad, master, mom_one, mom_two, *earlier)
 
@@ -417,10 +424,15 @@
         clip = clip_factor(part, n_dev, clip_norm)
         new_up, new_down = (), ()
         up_shards, down_shards = [], []
+        first_shard, = adamw(clip, rows_up[0], master_up, mom1_up, mom2_up, 0, (192, FF), (), True, False)
+        later = after(clip, first_shard)
         for layer in range(layers):
-            *new_up, shard = adamw(clip, rows_up[layer], master_up, mom1_up, mom2_up, layer, (96, FF), new_up)
+            if layer == 0:
+                new_up, shard = adamw(later, rows_up[0], master_up, mom1_up, mom2_up, 0, (192, FF), (), False, True), first_shard
+            else:
+                *new_up, shard = adamw(later, rows_up[layer], master_up, mom1_up, mom2_up, layer, (192, FF), new_up)
             up_shards.append(shard)
-            *new_down, shard = adamw(clip, rows_down[layer], master_down, mom1_down, mom2_down, layer, (48, width), new_down)
+            *new_down, shard = adamw(later, rows_down[layer], master_down, mom1_down, mom2_down, layer, (96, width), new_down)
             down_shards.append(shard)
         hidden = x_next.reshape(-1, width)
         for layer in range(layers):

time: 1270 us -> 1260 us (level)
    pallas_call x9 -> x10, Pallas kernels: 117 us -> 114 us  [the longest x5 74.7 us: adamw(): pl.pallas_call(functools.partial(adamw_kernel, len(earlier), weight, stat...]
  transfers between devices with their start and end apart: 14 -> 14, of which waited for: 5 -> 5; matrix products, arithmetic and copies ran while one was open for 0% -> 0% of each run, Pallas kernels for 70% -> 71%
where the time goes in v3:
time: 1260 us; the launch traced here: 1250 us
  Pallas kernels  1060 us (84%)
  waiting for transfers between devices  151 us (12%)
  starting transfers between devices  25.6 us (2%)
  between operations  14.3 us (1%)
    pallas_call x5, Pallas kernels, token_dot(): pl.pallas_call(token_dot_kernel, out_shape=jax.ShapeDtypeStruct((rows, co...  299 us
    pallas_call x4, Pallas kernels, act_and_dpre(): pl.pallas_call(act_dpre_kernel, out_shape=[jax.ShapeDtypeStruct((tokens,...  277 us
    pallas_call x2, Pallas kernels, forward_up(): pl.pallas_call(up_kernel, out_shape=jax.ShapeDtypeStruct((tokens, ff), jn...  143 us
    pallas_call x3, Pallas kernels, forward_down(): pl.pallas_call(down_kernel, out_shape=jax.ShapeDtypeStruct(hidden.shape,...  142 us
    pallas_call x2, Pallas kernels, grad_back(): pl.pallas_call(functools.partial(back_kernel, parts, bool(extra)), out_sh...  76.1 us
    pallas_call x5, Pallas kernels, adamw(): pl.pallas_call(functools.partial(adamw_kernel, len(earlier), weight, stat...  74.7 us
    all_to_all x2, waiting for transfers between devices, gradient_rows(): recv_up = lax.all_to_all(part_up, 'fsdp', 0, 0, tiled=True)  72.6 us
    all_gather x2, waiting for transfers between devices, local_step(): lax.all_gather(up_shards[layer], 'fsdp', axis=0, tiled=True)  53.5 us
  transfers between devices with their start and end apart: 14, of which 5 were waited for; matrix products, arithmetic and copies ran while one was open for 0% of the time, Pallas kernels for 71%

profile of v3, /device:TPU:0, one launch (start us, length us, event | category | flops | bytes accessed | tf_op | source)
XLA Modules:
  0.0 1253.5 jit_solution(12793747215779938865)
XLA Ops:
  8.1 69.2 %act_dpre.4 = (bf16[3072,3072]{1,0:T(8,128)(2,1)}, bf16[3072,3072]{1,0:T(8,128)(2,1)}) custom-call(s32[1]{0:T(128)} %bitcast.1.core_ref.order_ref, bf16[6144,1536]{1,0:T(8,128)(2,1)} %bitcast.32, bf16[3072,1536]{1,0:T(8,128)(2,1)} %bitcast.23, bf16[2,1536,6144]{2,1,0:T(8,128)(2,1)} %up_ref.7, bf16[2,6144,1536]{2,1,0:T(8,128)(2,1)} %down_ref.7), custom_call_target="tpu_custom_call" | custom-call | flops 57982058496 | bytes 113246208 | tf_op jit(solution)/shard_map/act_dpre/pallas_call | solution.py:76
  77.3 69.5 %act_dpre.5 = (bf16[3072,3072]{1,0:T(8,128)(2,1)}, bf16[3072,3072]{1,0:T(8,128)(2,1)}) custom-call(s32[1]{0:T(128)} %bitcast.1.core_ref.order_ref, bf16[6144,1536]{1,0:T(8,128)(2,1)} %collective-permute-done.x_ref.left_peer, bf16[3072,1536]{1,0:T(8,128)(2,1)} %collective-permute-done.1.g_ref.right_peer, bf16[2,1536,6144]{2,1,0:T(8,128)(2,1)} %up_ref.7, ...), custom_call_target="tpu_custom_call" | custom-call | flops 57982058496 | bytes 113246208 | tf_op jit(solution)/shard_map/act_dpre/pallas_call | solution.py:76
  146.7 37.0 %grad_back.2 = f32[3072,1536]{1,0:T(8,128)} custom-call(s32[1]{0:T(128)} %bitcast.1.core_ref.order_ref, bf16[3072,3072]{1,0:T(8,128)(2,1)} %get-tuple-element.52.right_peer.dpre_ref, bf16[2,1536,6144]{2,1,0:T(8,128)(2,1)} %up_ref.7, bf16[2,1536,6144]{2,1,0:T(8,128)(2,1)} %up_ref.7, bf16[2,1536,6144]{2,1,0:T(8,128)(2,1)} %up_ref.7, bf16[2,1536,6144]{2,1,0:T(8,128)(2,1)} %up_ref.7), custom_call_target="tpu_custom_call" | custom-call | flops 28991029248 | bytes 66060288 | tf_op jit(solution)/shard_map/grad_back/pallas_call | solution.py:112
  184.2 80.6 %token_dot.5 = bf16[3072,1536]{1,0:T(8,128)(2,1)} custom-call(s32[1]{0:T(128)} %bitcast.1.core_ref.order_ref, bf16[3072,3072]{1,0:T(8,128)(2,1)} %get-tuple-element.46.left_own, bf16[3072,1536]{1,0:T(8,128)(2,1)} %bitcast.24, bf16[3072,3072]{1,0:T(8,128)(2,1)} %get-tuple-element.48.left_peer, bf16[3072,1536]{1,0:T(8,128)(2,1)} %collective-permute-done.1.g_ref.right_peer), custom_call_target="tpu_custom_call" | custom-call | flops 57982058496 | bytes 66060288 | tf_op jit(solution)/shard_map/token_dot/pallas_call | solution.py:163
  264.8 5.8 all-to-all-start
  270.6 39.2 %grad_back.3.g_ref.right_own = bf16[3072,1536]{1,0:T(8,128)(2,1)} custom-call(s32[1]{0:T(128)} %bitcast.1.core_ref.order_ref, bf16[3072,3072]{1,0:T(8,128)(2,1)} %get-tuple-element.51.right_own.dpre_ref, bf16[2,1536,6144]{2,1,0:T(8,128)(2,1)} %up_ref.7, bf16[2,1536,6144]{2,1,0:T(8,128)(2,1)} %up_ref.7, bf16[2,1536,6144]{2,1,0:T(8,128)(2,1)} %up_ref.7, ...), custom_call_target="tpu_custom_call" | custom-call | flops 28991029248 | bytes 66060288 | tf_op jit(solution)/shard_map/grad_back/pallas_call | solution.py:112
  309.9 70.0 %token_dot.6 = bf16[1536,3072]{1,0:T(8,128)(2,1)} custom-call(s32[1]{0:T(128)} %bitcast.1.core_ref.order_ref, bf16[6144,1536]{1,0:T(8,128)(2,1)} %bitcast.33, bf16[3072,3072]{1,0:T(8,128)(2,1)} %get-tuple-element.51.right_own.dpre_ref, bf16[6144,1536]{1,0:T(8,128)(2,1)} %collective-permute-done.x_ref.left_peer, ...), custom_call_target="tpu_custom_call" | custom-call | flops 57982058496 | bytes 66060288 | tf_op jit(solution)/shard_map/token_dot/pallas_call | solution.py:163
  383.8 69.1 %act_dpre.6 = (bf16[3072,3072]{1,0:T(8,128)(2,1)}, bf16[3072,3072]{1,0:T(8,128)(2,1)}) custom-call(s32[1]{0:T(128)} %bitcast.1.core_ref.order_ref, bf16[6144,1536]{1,0:T(8,128)(2,1)} %bitcast.34, bf16[3072,1536]{1,0:T(8,128)(2,1)} %grad_back.3.g_ref.right_own, bf16[2,1536,6144]{2,1,0:T(8,128)(2,1)} %up_ref.7, bf16[2,6144,1536]{2,1,0:T(8,128)(2,1)} %down_ref.7), custom_call_target="tpu_custom_call" | custom-call | flops 57982058496 | bytes 113246208 | tf_op jit(solution)/shard_map/act_dpre/pallas_call | solution.py:76
  452.8 69.3 %act_dpre.7 = (bf16[3072,3072]{1,0:T(8,128)(2,1)}, bf16[3072,3072]{1,0:T(8,128)(2,1)}) custom-call(s32[1]{0:T(128)} %bitcast.1.core_ref.order_ref, bf16[6144,1536]{1,0:T(8,128)(2,1)} %collective-permute-done.x_ref.left_peer, bf16[3072,1536]{1,0:T(8,128)(2,1)} %collective-permute-done.3.g_ref.right_peer, bf16[2,1536,6144]{2,1,0:T(8,128)(2,1)} %up_ref.7, ...), custom_call_target="tpu_custom_call" | custom-call | flops 57982058496 | bytes 113246208 | tf_op jit(solution)/shard_map/act_dpre/pallas_call | solution.py:76
  522.2 28.0 %token_dot.7 = bf16[3072,512]{1,0:T(8,128)(2,1)} custom-call(s32[1]{0:T(128)} %bitcast.1.core_ref.order_ref, bf16[3072,3072]{1,0:T(8,128)(2,1)} %get-tuple-element.54.left_own, bf16[3072,1536]{1,0:T(8,128)(2,1)} %grad_back.3.g_ref.right_own, bf16[3072,3072]{1,0:T(8,128)(2,1)} %get-tuple-element.56.left_peer, ...), custom_call_target="tpu_custom_call" | custom-call | flops 19327352832 | bytes 47185920 | tf_op jit(solution)/shard_map/token_dot/pallas_call | solution.py:163
  555.4 49.6 %token_dot.8 = bf16[3072,1024]{1,0:T(8,128)(2,1)} custom-call(s32[1]{0:T(128)} %bitcast.1.core_ref.order_ref, bf16[3072,3072]{1,0:T(8,128)(2,1)} %get-tuple-element.54.left_own, bf16[3072,1536]{1,0:T(8,128)(2,1)} %grad_back.3.g_ref.right_own, bf16[3072,3072]{1,0:T(8,128)(2,1)} %get-tuple-element.56.left_peer, ...), custom_call_target="tpu_custom_call" | custom-call | flops 38654705664 | bytes 56623104 | tf_op jit(solution)/shard_map/token_dot/pallas_call | solution.py:163
  605.0 5.3 all-to-all-start.3
  610.3 70.4 %token_dot.9 = bf16[1536,3072]{1,0:T(8,128)(2,1)} custom-call(s32[1]{0:T(128)} %bitcast.1.core_ref.order_ref, bf16[6144,1536]{1,0:T(8,128)(2,1)} %bitcast.35, bf16[3072,3072]{1,0:T(8,128)(2,1)} %get-tuple-element.62.right_own, bf16[6144,1536]{1,0:T(8,128)(2,1)} %collective-permute-done.x_ref.left_peer, bf16[3072,3072]{1,0:T(8,128)(2,1)} %get-tuple-element.63.right_peer), custom_call_target="tpu_custom_call" | custom-call | flops 57982058496 | bytes 66060288 | tf_op jit(solution)/shard_map/token_dot/pallas_call | solution.py:163
  684.6 11.1 grad_sum.5
  696.4 7.8 grad_sum.6
  708.6 7.8 grad_sum.8
  717.1 72.6 %all-to-all-done.4 = bf16[8,192,3072]{2,1,0:T(8,128)(2,1)} async-done(((bf16[8,192,3072]{2,1,0:T(8,128)(2,1)}), bf16[8,192,3072]{2,1,0:T(8,128)(2,1)}, u32[]{:S(2)}, u32[]{:S(2)}) %all-to-all-start.4) | async-done | bytes 9437216 | tf_op jit(solution)/shard_map/all_to_all | solution.py:403
  789.8 7.8 grad_sum.9
  798.9 6.1 clip_norm.1.refs_0_
  805.0 13.0 %adamw.5 = bf16[192,6144]{1,0:T(8,128)(2,1)} custom-call(f32[8,128]{1,0:T(8,128)} %clip_norm.1.refs_0_, f32[192,6144]{1,0:T(8,128)} %get-tuple-element.65.refs_1_, f32[2,192,6144]{2,1,0:T(8,128)} %refs_2_.12, f32[2,192,6144]{2,1,0:T(8,128)} %refs_3_.12, f32[2,192,6144]{2,1,0:T(8,128)} %refs_4_.8), custom_call_target="tpu_custom_call" | custom-call | flops 23592960 | bytes 18874368 | tf_op jit(solution)/shard_map/adamw/pallas_call | solution.py:290
  818.1 15.6 %adamw.6 = (f32[2,768,1536]{2,1,0:T(8,128)}, f32[2,768,1536]{2,1,0:T(8,128)}, f32[2,768,1536]{2,1,0:T(8,128)}, bf16[768,1536]{1,0:T(8,128)(2,1)}) custom-call(f32[8,128]{1,0:T(8,128)} %clip_norm.1.refs_0_, f32[768,1536]{1,0:T(8,128)} %get-tuple-element.67.refs_1_, f32[2,768,1536]{2,1,0:T(8,128)} %refs_2_.13, f32[2,768,1536]{2,1,0:T(8,128)} %refs_3_.13, ...), custom_call_target="tpu_custom_call" | custom-call | flops 23592960 | bytes 33030144 | tf_op jit(solution)/shard_map/adamw/pallas_call | solution.py:290
  833.8 14.8 %adamw.7 = (f32[2,192,6144]{2,1,0:T(8,128)}, f32[2,192,6144]{2,1,0:T(8,128)}, f32[2,192,6144]{2,1,0:T(8,128)}) custom-call(f32[8,128]{1,0:T(8,128)} %clip_norm.1.refs_0_, f32[192,6144]{1,0:T(8,128)} %get-tuple-element.65.refs_1_, f32[2,192,6144]{2,1,0:T(8,128)} %refs_2_.12, f32[2,192,6144]{2,1,0:T(8,128)} %refs_3_.12, f32[2,192,6144]{2,1,0:T(8,128)} %refs_4_.8), custom_call_target="tpu_custom_call" | custom-call | flops 23592960 | bytes 33030144 | tf_op jit(solution)/shard_map/adamw/pallas_call | solution.py:290
  848.6 15.6 %adamw.8 = (f32[2,192,6144]{2,1,0:T(8,128)}, f32[2,192,6144]{2,1,0:T(8,128)}, f32[2,192,6144]{2,1,0:T(8,128)}, bf16[192,6144]{1,0:T(8,128)(2,1)}) custom-call(f32[8,128]{1,0:T(8,128)} %clip_norm.1.refs_0_, f32[192,6144]{1,0:T(8,128)} %get-tuple-element.69.refs_1_, ...), custom_call_target="tpu_custom_call", output_to_operand_aliasing={{0}: (5, {}), {1}: (6, {}), {2}: (7, {})} | custom-call | flops 23592960 | bytes 33030144 | tf_op jit(solution)/shard_map/adamw/pallas_call | solution.py:290
  864.3 15.6 %adamw.9 = (f32[2,768,1536]{2,1,0:T(8,128)}, f32[2,768,1536]{2,1,0:T(8,128)}, f32[2,768,1536]{2,1,0:T(8,128)}, bf16[768,1536]{1,0:T(8,128)(2,1)}) custom-call(f32[8,128]{1,0:T(8,128)} %clip_norm.1.refs_0_, f32[768,1536]{1,0:T(8,128)} %get-tuple-element.74.refs_1_, ...), custom_call_target="tpu_custom_call", output_to_operand_aliasing={{0}: (5, {}), {1}: (6, {}), {2}: (7, {})} | custom-call | flops 23592960 | bytes 33030144 | tf_op jit(solution)/shard_map/adamw/pallas_call | solution.py:290
  883.6 26.7 %all-gather.6.cloned.1.call-done.w_ref = bf16[1536,6144]{1,0:T(8,128)(2,1)} async-done(((bf16[192,6144]{1,0:T(8,128)(2,1)}), bf16[1536,6144]{1,0:T(8,128)(2,1)}) %all-gather.6.cloned.1.call-update) | async-done | bytes 18874384 | tf_op jit(solution)/shard_map/all_gather | solution.py:439
  910.3 71.4 %forward_up.2.act_ref = bf16[3072,6144]{1,0:T(8,128)(2,1)} custom-call(bf16[3072,1536]{1,0:T(8,128)(2,1)} %bitcast.36, bf16[1536,6144]{1,0:T(8,128)(2,1)} %all-gather.6.cloned.1.call-done.w_ref), custom_call_target="tpu_custom_call" | custom-call | flops 57982058496 | bytes 66060288 | tf_op jit(solution)/shard_map/forward_up/pallas_call | solution.py:316
  981.8 23.4 %all-gather.8.cloned.1.call-done.w_ref = bf16[6144,1536]{1,0:T(8,128)(2,1)} async-done(((bf16[768,1536]{1,0:T(8,128)(2,1)}), bf16[6144,1536]{1,0:T(8,128)(2,1)}) %all-gather.8.cloned.1.call-update) | async-done | bytes 18874384 | tf_op jit(solution)/shard_map/all_gather | solution.py:444
  1005.2 68.6 %forward_down.3.x_ref.hidden_ref = bf16[3072,1536]{1,0:T(8,128)(2,1)} custom-call(bf16[3072,6144]{1,0:T(8,128)(2,1)} %forward_up.2.act_ref, bf16[6144,1536]{1,0:T(8,128)(2,1)} %all-gather.8.cloned.1.call-done.w_ref, bf16[3072,1536]{1,0:T(8,128)(2,1)} %bitcast.37), custom_call_target="tpu_custom_call" | custom-call | flops 57982058496 | bytes 75497472 | tf_op jit(solution)/shard_map/forward_down/pallas_call | solution.py:351
  1073.8 26.8 %all-gather.10.cloned.1.call-done.w_ref = bf16[1536,6144]{1,0:T(8,128)(2,1)} async-done(((bf16[192,6144]{1,0:T(8,128)(2,1)}), bf16[1536,6144]{1,0:T(8,128)(2,1)}) %all-gather.10.cloned.1.call-update) | async-done | bytes 18874384 | tf_op jit(solution)/shard_map/all_gather | solution.py:439
  1100.6 71.5 %forward_up.3.act_ref = bf16[3072,6144]{1,0:T(8,128)(2,1)} custom-call(bf16[3072,1536]{1,0:T(8,128)(2,1)} %forward_down.3.x_ref.hidden_ref, bf16[1536,6144]{1,0:T(8,128)(2,1)} %all-gather.10.cloned.1.call-done.w_ref), custom_call_target="tpu_custom_call" | custom-call | flops 57982058496 | bytes 66060288 | tf_op jit(solution)/shard_map/forward_up/pallas_call | solution.py:316
  1172.0 36.4 %forward_down.4.refs_0_ = bf16[3072,1536]{1,0:T(8,128)(2,1)} custom-call(bf16[3072,6144]{1,0:T(8,128)(2,1)} %forward_up.3.act_ref, bf16[6144,768]{1,0:T(8,128)(2,1)} %all-gather.14.cloned.1.call-done.w_ref, bf16[3072,1536]{1,0:T(8,128)(2,1)} %forward_down.3.x_ref.hidden_ref), custom_call_target="tpu_custom_call" | custom-call | flops 28991029248 | bytes 56623104 | tf_op jit(solution)/shard_map/forward_down/pallas_call | solution.py:351
  1209.8 36.7 %forward_down.5 = bf16[3072,1536]{1,0:T(8,128)(2,1)} custom-call(bf16[3072,6144]{1,0:T(8,128)(2,1)} %forward_up.3.act_ref, bf16[6144,768]{1,0:T(8,128)(2,1)} %all-gather.12.cloned.1.call-done.w_ref, bf16[3072,1536]{1,0:T(8,128)(2,1)} %forward_down.3.x_ref.hidden_ref, bf16[3072,1536]{1,0:T(8,128)(2,1)} %forward_down.4.refs_0_), custom_call_target="tpu_custom_call", output_to_operand_aliasing={{}: (3, {})} | custom-call | flops 28991029248 | bytes 56623104 | tf_op jit(solution)/shard_map/forward_down/pallas_call | solution.py:351
  (39 shorter events, 26.8 us)
Async XLA Ops:
  7.2 70.1 %collective-permute-start = (bf16[6144,1536]{1,0:T(8,128)(2,1)}, bf16[6144,1536]{1,0:T(8,128)(2,1)}, u32[]{:S(2)}, u32[]{:S(2)}) collective-permute-start(bf16[6144,1536]{1,0:T(8,128)(2,1)} %bitcast.31), channel_id=1, source_target_pairs={{0,1},{1,0},{2,3},{3,2},{4,5},{5,4},{6,7},{7,6}} | collective-permute-start | bytes 56623112 | tf_op jit(solution)/shard_map/ppermute | solution.py:366
  8.0 69.2 %collective-permute-start.1 = (bf16[3072,1536]{1,0:T(8,128)(2,1)}, bf16[3072,1536]{1,0:T(8,128)(2,1)}, u32[]{:S(2)}, u32[]{:S(2)}) collective-permute-start(bf16[3072,1536]{1,0:T(8,128)(2,1)} %bitcast.22), channel_id=1, source_target_pairs={{0,1},{1,0},{2,3},{3,2},{4,5},{5,4},{6,7},{7,6}} | collective-permute-start | bytes 28311560 | tf_op jit(solution)/shard_map/ppermute | solution.py:366
  183.7 86.9 %collective-permute-start.2 = (f32[3072,1536]{1,0:T(8,128)}, f32[3072,1536]{1,0:T(8,128)}, u32[]{:S(2)}, u32[]{:S(2)}) collective-permute-start(f32[3072,1536]{1,0:T(8,128)} %grad_back.2), channel_id=1, source_target_pairs={{0,1},{1,0},{2,3},{3,2},{4,5},{5,4},{6,7},{7,6}} | collective-permute-start | bytes 56623112 | tf_op jit(solution)/shard_map/ppermute | solution.py:366
  264.8 115.0 %all-to-all-start = ((bf16[4,768,1536]{2,1,0:T(8,128)(2,1)}), bf16[4,768,1536]{2,1,0:T(8,128)(2,1)}, u32[]{:S(2)}, u32[]{:S(2)}) async-start(bf16[4,768,1536]{2,1,0:T(8,128)(2,1)} %bitcast.27), calls=%async_computation | async-start | bytes 18874368 | tf_op jit(solution)/shard_map/all_to_all | solution.py:397
  309.8 143.0 %collective-permute-start.3 = (bf16[3072,1536]{1,0:T(8,128)(2,1)}, bf16[3072,1536]{1,0:T(8,128)(2,1)}, u32[]{:S(2)}, u32[]{:S(2)}) collective-permute-start(bf16[3072,1536]{1,0:T(8,128)(2,1)} %grad_back.3.g_ref.right_own), channel_id=1, source_target_pairs={{0,1},{1,0},{2,3},{3,2},{4,5},{5,4},{6,7},{7,6}} | collective-permute-start | bytes 28311560 | tf_op jit(solution)/shard_map/ppermute | solution.py:366
  379.9 170.3 %all-to-all-start.1 = ((bf16[8,192,3072]{2,1,0:T(8,128)(2,1)}), bf16[8,192,3072]{2,1,0:T(8,128)(2,1)}, u32[]{:S(2)}, u32[]{:S(2)}) async-start(bf16[8,192,3072]{2,1,0:T(8,128)(2,1)} %bitcast.28), calls=%async_computation.1 | async-start | bytes 18874368 | tf_op jit(solution)/shard_map/all_to_all | solution.py:403
  550.2 54.8 %all-to-all-start.2 = ((bf16[4,768,512]{2,1,0:T(8,128)(2,1)}), bf16[4,768,512]{2,1,0:T(8,128)(2,1)S(1)}, u32[]{:S(2)}, u32[]{:S(2)}) async-start(bf16[4,768,512]{2,1,0:T(8,128)(2,1)} %bitcast.30), calls=%async_computation.2 | async-start | bytes 6291456 | tf_op jit(solution)/shard_map/all_to_all | solution.py:397
  605.0 75.7 %copy-start = (bf16[4,768,512]{2,1,0:T(8,128)(2,1)}, bf16[4,768,512]{2,1,0:T(8,128)(2,1)S(1)}, u32[]{:S(2)}) copy-start(bf16[4,768,512]{2,1,0:T(8,128)(2,1)S(1)} %all-to-all-done.2.recv_ref) | copy-start | bytes 9437188
  605.0 75.7 %all-to-all-start.3 = ((bf16[4,768,1024]{2,1,0:T(8,128)(2,1)}), bf16[4,768,1024]{2,1,0:T(8,128)(2,1)}, u32[]{:S(2)}, u32[]{:S(2)}) async-start(bf16[4,768,1024]{2,1,0:T(8,128)(2,1)} %bitcast.29), calls=%async_computation.3 | async-start | bytes 12582912 | tf_op jit(solution)/shard_map/all_to_all | solution.py:397
  680.7 109.0 %all-to-all-start.4 = ((bf16[8,192,3072]{2,1,0:T(8,128)(2,1)}), bf16[8,192,3072]{2,1,0:T(8,128)(2,1)}, u32[]{:S(2)}, u32[]{:S(2)}) async-start(bf16[8,192,3072]{2,1,0:T(8,128)(2,1)} %bitcast.26), calls=%async_computation.4 | async-start | bytes 18874368 | tf_op jit(solution)/shard_map/all_to_all | solution.py:403
  684.5 225.8 %all-gather.6.cloned.1.call-start = ((), (), s32[]{:S(2)}) async-start(), calls=%async_computation.5 | async-start | bytes 21233664 | tf_op jit(solution)/shard_map/all_gather | solution.py:439
  708.6 7.8 copy-start.2
  789.8 7.8 copy-start.1
  818.1 187.1 %all-gather.8.cloned.1.call-start = ((), (), s32[]{:S(2)}) async-start(), calls=%async_computation.6 | async-start | bytes 21233664 | tf_op jit(solution)/shard_map/all_gather | solution.py:444
  833.7 266.8 %all-gather.10.cloned.1.call-start = ((), (), s32[]{:S(2)}) async-start(), calls=%async_computation.7 | async-start | bytes 21233664 | tf_op jit(solution)/shard_map/all_gather | solution.py:439
  864.2 307.8 %all-gather.14.cloned.1.call-start = ((), (), s32[]{:S(2)}) async-start(), calls=%async_computation.9 | async-start | bytes 10616832 | tf_op jit(solution)/shard_map/all_gather | solution.py:444
  883.1 326.8 %all-gather.12.cloned.1.call-start = ((), (), s32[]{:S(2)}) async-start(), calls=%async_computation.8 | async-start | bytes 10616832 | tf_op jit(solution)/shard_map/all_gather | solution.py:444
Sparse Core Ops, SparseCore 0:
  818.2 92.1 all-gather.5
  912.2 92.9 all-gather.7
  1007.5 92.9 all-gather.9
  1102.2 52.9 all-gather.13
  1156.9 52.9 all-gather.11
